TPU v7x, 32 devices: a whole 2x2x4 slice. The times are simulated.
32 devices in a mesh: ctx: 4 (over y, x), fsdp: 8 (over z, core).
Axes of the slice: x: 2, y: 2, z: 4, core: 2. Of those that a mesh axis runs over, the one named last changes fastest.
Arguments:
- query_a: bfloat16 [8, 512, 2048], P('fsdp', 'ctx'), may hold values from -64 to 64
- key_a: bfloat16 [8, 512, 256], P('fsdp', 'ctx'), may hold values from -8 to 8
- value_a: bfloat16 [8, 512, 256], P('fsdp', 'ctx'), may hold values from -6 to 6
- resid_in: bfloat16 [8, 512, 1440], P('fsdp', 'ctx'), may hold values from -6 to 6
- doc_lengths: int32 [8, 6], P('fsdp'), may hold values from 1 to 384, 512 in all within a row
- w_out: bfloat16 [2048, 1440], P('fsdp'), may hold values from -0.125 to 0.125
- w_qkv: bfloat16 [1440, 2560], P('fsdp'), may hold values from -8 to 8
- grad_out: bfloat16 [8, 512, 2048], P('fsdp', 'ctx'), may hold values from -6 to 6
- grad_resid: bfloat16 [8, 512, 1440], P('fsdp', 'ctx'), may hold values from -8 to 8
Outputs:
- banded_out: bfloat16 [8, 512, 2048], P('fsdp', 'ctx')
- grad_input: bfloat16 [8, 512, 1440], P('fsdp', 'ctx')
- grad_query: bfloat16 [8, 512, 2048], P('fsdp', 'ctx')
- grad_key: bfloat16 [8, 512, 256], P('fsdp', 'ctx')
- grad_value: bfloat16 [8, 512, 256], P('fsdp', 'ctx')
- grad_w_out: float32 [2048, 1440], P('fsdp')
- grad_w_qkv: float32 [1440, 2560], P('fsdp')
Inputs may be any that keep to these rules, and one draw needn't show every extreme that they name: `doc_lengths`: the lengths of a sequence sum to 512, and one document has 384 positions.
All inputs are finite; a program needn't handle non-finite values.
Results may differ from a plain program's by a relative error of at most 0.03.
Values may be sent and summed in bfloat16 or wider, within the bound.
A program may use at most 128 MiB of HBM per device.

v0:
```python
import functools

import jax
import jax.numpy as jnp
from jax import lax
from jax.experimental import pallas as pl
from jax.experimental.pallas import tpu as pltpu
from jax.sharding import PartitionSpec as P

H = 32
KV = 4
DH = 64
BAND = 128


MASKED = -1e30
EPSILON = 1e-05


def from_behind(value, axis, steps):
    count = lax.axis_size(axis)
    leading, last = (max(0, -steps), min(count, count - steps))
    return lax.ppermute(value, axis, [(source, source + steps) for source in range(leading, last)])


def doc_table(lengths, seq_len):
    ends = jnp.cumsum(lengths)
    places = jnp.arange(seq_len, dtype=jnp.int32)
    before = places[:, None] >= ends[None, :]
    return jnp.sum(before.astype(jnp.int32), axis=1)


def attend_kernel(with_output, with_grads, *refs):
    refs = list(refs)
    allowed_ref, q_ref, k_ref, v_ref, v_t_ref = refs[:5]
    del refs[:5]
    if with_grads:
        k_t_ref, g_ref = refs[:2]
        del refs[:2]
    o_ref = refs.pop(0)
    if with_grads:
        dq_ref, dk_ref, dv_ref = refs
    allowed = allowed_ref[...] > 0.0
    keys, values, values_t = (k_ref[0], v_ref[0], v_t_ref[...])
    dk = jnp.zeros(keys.shape, jnp.float32)
    dv = jnp.zeros(keys.shape, jnp.float32)
    by_last = (((1,), (1,)), ((), ()))
    for head in range(H // KV):
        rows = slice(head * DH, (head + 1) * DH)
        query = q_ref[rows, :]
        scores = jnp.dot(keys, query, preferred_element_type=jnp.float32) * DH ** (-0.5)
        scores = jnp.where(allowed, scores, MASKED)
        row_max = jnp.max(scores, axis=0, keepdims=True)
        log_total = row_max + jnp.log(
            jnp.sum(jnp.exp(scores - row_max), axis=0, keepdims=True)
        )
        weights = jnp.where(allowed, jnp.exp(scores - log_total), 0.0)
        weights_bf = weights.astype(jnp.bfloat16)
        if with_output:
            output = jnp.dot(values_t, weights_bf, preferred_element_type=jnp.float32)
            output = output.astype(jnp.bfloat16)
            o_ref[rows, :] = output
        else:
            output = o_ref[rows, :]
        if with_grads:
            grad = g_ref[rows, :]
            correction = jnp.sum(
                grad.astype(jnp.float32) * output.astype(jnp.float32), axis=0, keepdims=True
            )
            grad_weights = jnp.dot(values, grad, preferred_element_type=jnp.float32)
            grad_scores = (weights * (grad_weights - correction)).astype(jnp.bfloat16)
            grad_q = jnp.dot(k_t_ref[...], grad_scores, preferred_element_type=jnp.float32)
            dq_ref[rows, :] = (grad_q * DH ** (-0.5)).astype(jnp.bfloat16)
            dk += lax.dot_general(grad_scores, query, by_last, preferred_element_type=jnp.float32)
            dv += lax.dot_general(weights_bf, grad, by_last, preferred_element_type=jnp.float32)
    if with_grads:
        dk_ref[0] = dk
        dv_ref[0] = dv


def by_head(rows):
    return rows.reshape(rows.shape[0], KV, DH).transpose(1, 0, 2)


def from_heads(heads):
    return heads.transpose(1, 0, 2).reshape(heads.shape[1], KV * DH)


def attend(allowed_t, query_t, keys, values, output_t=None, grad_t=None):
    columns, rows = allowed_t.shape
    with_output, with_grads = (output_t is None, grad_t is not None)
    group = pl.BlockSpec((query_t.shape[0] // KV, rows), lambda g: (g, 0))
    key_rows = pl.BlockSpec((1, columns, DH), lambda g: (g, 0, 0))
    key_columns = pl.BlockSpec((DH, columns), lambda g: (g, 0))
    args = [allowed_t, query_t, by_head(keys), by_head(values), values.T]
    in_specs = [pl.BlockSpec((columns, rows), lambda g: (0, 0)), group]
    in_specs += [key_rows, key_rows, key_columns]
    out_shape, out_specs = ([], [])
    wide = jax.ShapeDtypeStruct(query_t.shape, jnp.bfloat16)
    narrow = jax.ShapeDtypeStruct((KV, columns, DH), jnp.float32)
    if with_grads:
        args += [keys.T, grad_t]
        in_specs += [key_columns, group]
    if with_output:
        out_shape.append(wide)
        out_specs.append(group)
    else:
        args.append(output_t)
        in_specs.append(group)
    if with_grads:
        out_shape += [wide, narrow, narrow]
        out_specs += [group, key_rows, key_rows]
    return pl.pallas_call(
        functools.partial(attend_kernel, with_output, with_grads),
        grid=(KV,),
        out_shape=tuple(out_shape),
        in_specs=in_specs,
        out_specs=tuple(out_specs),
    )(*args)


MESH = pl.DeviceIdType.MESH


def remote(src, dst, send_sem, recv_sem, ctx, fsdp):
    return pltpu.make_async_remote_copy(
        src_ref=src,
        dst_ref=dst,
        send_sem=send_sem,
        recv_sem=recv_sem,
        device_id={"ctx": ctx, "fsdp": fsdp},
        device_id_type=MESH,
    )


def place():
    return (lax.axis_index("ctx"), lax.axis_index("fsdp"))


def shard_at(z, core, planes, offset):
    return 2 * lax.rem(z + offset, planes) + core


def greet(planes):
    c, f = place()
    z, core = (f // 2, lax.rem(f, 2))
    barrier = pltpu.get_barrier_semaphore()
    peers = [(c ^ 1, f), (c ^ 2, f), (c ^ 3, f), (c, f ^ 1)]
    peers += [(c, shard_at(z, core, planes, d)) for d in range(1, planes)]
    for ctx, fsdp in peers:
        pl.semaphore_signal(
            barrier, inc=1, device_id={"ctx": ctx, "fsdp": fsdp}, device_id_type=MESH
        )
    pl.semaphore_wait(barrier, len(peers))


def quarter_of(ref, weight, quarter):
    if weight == 0:
        size = ref.shape[0] // 4
        return ref.at[pl.ds(pl.multiple_of(quarter * size, 16), size), :]
    size = ref.shape[1] // 4
    return ref.at[:, pl.ds(pl.multiple_of(quarter * size, 128), size)]


def by_distance(planes):
    order = []
    for step in range(1, planes // 2 + 1):
        for d in (step, planes - step):
            if d not in order:
                order.append(d)
    return order


def gather_kernel(
    planes, wo, wq, kv, go, gq, gkv, send, recv_z, recv_x, recv_y, recv_d, recv_p, recv_kv, local
):
    c, f = place()
    z, core = (f // 2, lax.rem(f, 2))
    mine, full = ((wo, wq), (go, gq))
    rows = kv.shape[0]
    owns = [
        pltpu.make_async_copy(kv, gkv.at[pl.ds(pl.multiple_of(c * rows, 128), rows)], local),
        pltpu.make_async_copy(wo, go.at[f], local),
        pltpu.make_async_copy(wq, gq.at[f], local),
    ]
    for copy in owns:
        copy.start()
    greet(planes)
    started = []

    def push(*args):
        copy = remote(*args)
        copy.start()
        started.append(copy)

    def piece(weight, shard, quarter):
        return quarter_of(full[weight].at[shard], weight, quarter)

    def arrive(ref, sem):
        remote(ref, ref, send, sem, c ^ 1, f).wait_recv()

    kv_place = gkv.at[pl.ds(pl.multiple_of(c * rows, 128), rows)]
    for i, bit in enumerate((1, 2, 3)):
        push(kv, kv_place, send, recv_kv.at[i], c ^ bit, f)
    order = by_distance(planes)
    for weight in (0, 1):
        for d in order:
            push(
                quarter_of(mine[weight], weight, c),
                piece(weight, f, c),
                send,
                recv_z.at[weight, d],
                c,
                shard_at(z, core, planes, d),
            )
        push(mine[weight], full[weight].at[f], send, recv_p.at[weight, 0, 0], c, f ^ 1)
    steps = [(weight, d) for weight in (0, 1) for d in order]

    def to_partner(weight, d, shard, slot):
        part = piece(weight, shard, c ^ slot)
        push(part, part, send, recv_p.at[weight, d, slot], c, f ^ 1)

    def first(weight, d):
        shard = shard_at(z, core, planes, planes - d)
        part = piece(weight, shard, c)
        arrive(part, recv_z.at[weight, d])
        push(part, part, send, recv_x.at[weight, d], c ^ 1, f)
        push(part, part, send, recv_y.at[weight, d], c ^ 2, f)
        to_partner(weight, d, shard, 0)

    def second(weight, d):
        shard = shard_at(z, core, planes, planes - d)
        arrive(piece(weight, shard, c ^ 1), recv_x.at[weight, d])
        arrive(piece(weight, shard, c ^ 2), recv_y.at[weight, d])
        bit = jnp.where(core == weight, 1, 2)
        part = piece(weight, shard, c ^ bit)
        push(part, part, send, recv_d.at[weight, d], c ^ (3 - bit), f)
        to_partner(weight, d, shard, 1)
        to_partner(weight, d, shard, 2)

    def third(weight, d):
        shard = shard_at(z, core, planes, planes - d)
        arrive(piece(weight, shard, c ^ 3), recv_d.at[weight, d])
        to_partner(weight, d, shard, 3)

    count = len(steps)
    for i in range(count + 2):
        if i < count:
            first(*steps[i])
        if 0 <= i - 1 < count:
            second(*steps[i - 1])
        if 0 <= i - 2 < count:
            third(*steps[i - 2])
    for weight in (0, 1):
        arrive(full[weight].at[f ^ 1], recv_p.at[weight, 0, 0])
        for d in order:
            shard = shard_at(z, core, planes, planes - d) ^ 1
            for slot in range(4):
                arrive(piece(weight, shard, c ^ slot), recv_p.at[weight, d, slot])
    for i in range(3):
        arrive(kv_place, recv_kv.at[i])
    for copy in started:
        copy.wait_send()
    for copy in owns:
        copy.wait()


def gather_weights(w_out, w_qkv, kv):
    count = lax.axis_size("fsdp")
    planes = count // 2
    dma = pltpu.SemaphoreType.DMA
    anywhere = pl.BlockSpec(memory_space=pl.ANY)
    return pl.pallas_call(
        functools.partial(gather_kernel, planes),
        out_shape=(
            jax.ShapeDtypeStruct((count,) + w_out.shape, w_out.dtype),
            jax.ShapeDtypeStruct((count,) + w_qkv.shape, w_qkv.dtype),
            jax.ShapeDtypeStruct((4 * kv.shape[0], kv.shape[1]), kv.dtype),
        ),
        in_specs=[anywhere] * 3,
        out_specs=(anywhere,) * 3,
        scratch_shapes=[
            dma,
            dma((2, planes)),
            dma((2, planes)),
            dma((2, planes)),
            dma((2, planes)),
            dma((2, planes, 4)),
            dma((3,)),
            dma,
        ],
        compiler_params=pltpu.CompilerParams(collective_id=0, has_side_effects=True),
    )(w_out, w_qkv, kv)


def reduce_kernel(
    planes,
    att_t,
    norm_t,
    grad_mid,
    grad_proj,
    kv_sums,
    out_o,
    out_q,
    out_kv,
    a_o,
    a_q,
    s_o,
    s_q,
    p_o,
    p_q,
    r1_o,
    r1_q,
    r2_o,
    r2_q,
    rz_o,
    rz_q,
    from_kv,
    send,
    recv_p,
    recv_1,
    recv_2,
    recv_z,
    recv_f,
    recv_kv,
):
    c, f = place()
    z, core = (f // 2, lax.rem(f, 2))
    greet(planes)
    own, sent, from_p, from_1, from_2, from_z, result = (
        (a_o, a_q),
        (s_o, s_q),
        (p_o, p_q),
        (r1_o, r1_q),
        (r2_o, r2_q),
        (rz_o, rz_q),
        (out_o, out_q),
    )
    started = []

    def push(*args):
        copy = remote(*args)
        copy.start()
        started.append(copy)

    def arrive(ref, sem):
        remote(ref, ref, send, sem, c ^ 1, f).wait_recv()

    def term(weight, shard):
        if weight == 0:
            size = a_o.shape[1]
            left = att_t[pl.ds(pl.multiple_of(shard * size, size), size), :]
            right = grad_mid[...]
        else:
            left = norm_t[shard]
            right = grad_proj[...]
        return jnp.dot(left, right, preferred_element_type=jnp.float32).astype(jnp.bfloat16)

    def added(first, second):
        return (first.astype(jnp.float32) + second.astype(jnp.float32)).astype(jnp.bfloat16)

    rows = out_kv.shape[0]

    def kv_rows(index):
        return kv_sums.at[pl.ds(pl.multiple_of(index * rows, rows), rows), :]

    for slot in (3, 1, 2):
        push(
            kv_rows(c ^ slot), from_kv.at[slot], send, recv_kv.at[slot], c ^ slot, f
        )
    order = by_distance(planes)[::-1] + [0]
    steps = [(weight, d) for d in order for weight in (1, 0)]

    def bits(weight):
        bit = jnp.where(core == weight, 1, 2)
        return (bit, 3 - bit)

    def produce(weight, d):
        shard = shard_at(z, core, planes, d)
        sent[weight][d] = term(weight, shard ^ 1)
        push(sent[weight].at[d], from_p[weight].at[d], send, recv_p.at[weight, d], c, f ^ 1)
        own[weight][d] = term(weight, shard)

    def chip_sum(weight, d):
        arrive(from_p[weight].at[d], recv_p.at[weight, d])
        own[weight][d] = added(own[weight][d], from_p[weight][d])
        bit, other = bits(weight)
        for slot, quarter in ((1, c ^ 3), (0, c ^ bit)):
            push(
                quarter_of(own[weight].at[d], weight, quarter),
                from_1[weight].at[d, slot],
                send,
                recv_1.at[weight, d, slot],
                c ^ bit,
                f,
            )

    def pair_sum(weight, d):
        bit, other = bits(weight)
        for slot, quarter in ((1, c ^ other), (0, c)):
            arrive(from_1[weight].at[d, slot], recv_1.at[weight, d, slot])
            part = quarter_of(own[weight].at[d], weight, quarter)
            part[...] = added(part[...], from_1[weight][d, slot])
            if slot == 1:
                push(part, from_2[weight].at[d], send, recv_2.at[weight, d], c ^ other, f)

    def plane_sum(weight, d):
        arrive(from_2[weight].at[d], recv_2.at[weight, d])
        part = quarter_of(own[weight].at[d], weight, c)
        part[...] = added(part[...], from_2[weight][d])
        if d:
            push(
                part,
                from_z[weight].at[d],
                send,
                recv_z.at[weight, d],
                c,
                shard_at(z, core, planes, d),
            )

    def finish(weight):
        part = quarter_of(own[weight].at[0], weight, c)
        total = part[...].astype(jnp.float32)
        for d in range(1, planes):
            arrive(from_z[weight].at[d], recv_z.at[weight, d])
            total = total + from_z[weight][d].astype(jnp.float32)
        place_c = quarter_of(result[weight], weight, c)
        place_c[...] = total.astype(jnp.bfloat16)
        for slot in (3, 1, 2):
            push(place_c, place_c, send, recv_f.at[weight, slot], c ^ slot, f)

    stages = (produce, chip_sum, pair_sum, plane_sum)
    lags = (0, 2, 4, 6)
    count = len(steps)
    for i in range(count + lags[-1]):
        for stage, lag in zip(stages, lags):
            if 0 <= i - lag < count:
                stage(*steps[i - lag])
    kv_total = kv_rows(c)[...].astype(jnp.float32)
    for slot in (1, 2, 3):
        arrive(from_kv.at[slot], recv_kv.at[slot])
        kv_total += from_kv[slot].astype(jnp.float32)
    out_kv[...] = kv_total
    for weight in (1, 0):
        finish(weight)
    for weight in (1, 0):
        for slot in (3, 1, 2):
            arrive(quarter_of(result[weight], weight, c ^ slot), recv_f.at[weight, slot])
    for copy in started:
        copy.wait_send()


def reduce_weights(att_t, norm_t, grad_mid, grad_proj, kv_sums):
    count = lax.axis_size("fsdp")
    planes = count // 2
    dma = pltpu.SemaphoreType.DMA
    in_vmem = pl.BlockSpec(memory_space=pltpu.VMEM)
    bf = jnp.bfloat16
    o_shape = (att_t.shape[0] // count, grad_mid.shape[1])
    q_shape = (norm_t.shape[1], grad_proj.shape[1])
    o_part = (o_shape[0] // 4, o_shape[1])
    q_part = (q_shape[0], q_shape[1] // 4)
    scratch = []
    for lead, shapes in (
        ((planes,), (o_shape, q_shape)),
        ((planes,), (o_shape, q_shape)),
        ((planes,), (o_shape, q_shape)),
        ((planes, 2), (o_part, q_part)),
        ((planes,), (o_part, q_part)),
        ((planes,), (o_part, q_part)),
    ):
        scratch += [pltpu.VMEM(lead + shape, bf) for shape in shapes]
    kv_shape = (kv_sums.shape[0] // 4, kv_sums.shape[1])
    scratch.append(pltpu.VMEM((4,) + kv_shape, bf))
    return pl.pallas_call(
        functools.partial(reduce_kernel, planes),
        out_shape=(
            jax.ShapeDtypeStruct(o_shape, bf),
            jax.ShapeDtypeStruct(q_shape, bf),
            jax.ShapeDtypeStruct(kv_shape, jnp.float32),
        ),
        in_specs=[in_vmem] * 5,
        out_specs=(in_vmem,) * 3,
        scratch_shapes=scratch
        + [
            dma,
            dma((2, planes)),
            dma((2, planes, 2)),
            dma((2, planes)),
            dma((2, planes)),
            dma((2, 4)),
            dma((4,)),
        ],
        compiler_params=pltpu.CompilerParams(
            collective_id=1, has_side_effects=True, vmem_limit_bytes=60 * 2**20
        ),
    )(att_t, norm_t, grad_mid, grad_proj, kv_sums)


def per_device(query_a, key_a, value_a, resid_in, doc_lengths, w_out, w_qkv, grad_out, grad_resid):
    ctx_count = lax.axis_size("ctx")
    ctx_index = lax.axis_index("ctx")
    local_rows = query_a.shape[1]
    seq_len = local_rows * ctx_count
    band_len = BAND
    first_row = ctx_index * local_rows
    documents = doc_table(doc_lengths[0], seq_len)
    fsdp_count = lax.axis_size("fsdp")
    own_kernels = ctx_count == 4 and fsdp_count % 2 == 0 and w_out.shape[0] % 64 == 0
    if own_kernels:
        w_o3, w_b3, kv = gather_weights(
            w_out, w_qkv, jnp.concatenate([key_a[0], value_a[0]], axis=1)
        )
        w_o = w_o3.reshape(-1, w_out.shape[1])
        w_b = w_b3.reshape(-1, w_qkv.shape[1])
        keys, values = (kv[:, : KV * DH], kv[:, KV * DH :])
    else:
        w_o, w_b = (
            lax.all_gather(w_out, "fsdp", axis=0, tiled=True),
            lax.all_gather(w_qkv, "fsdp", axis=0, tiled=True),
        )
        keys, values = (
            lax.all_gather(key_a[0], "ctx", axis=0, tiled=True),
            lax.all_gather(value_a[0], "ctx", axis=0, tiled=True),
        )
    query_t = query_a[0].T
    row_docs = lax.dynamic_slice_in_dim(documents, first_row, local_rows)[None, :]
    row_places = (first_row + jnp.arange(local_rows, dtype=jnp.int32))[None, :]
    columns = jnp.arange(seq_len, dtype=jnp.int32)[:, None]
    allowed_t = ((documents[:, None] == row_docs) & (columns <= row_places)).astype(jnp.float32)
    (attended_t,) = attend(allowed_t, query_t, keys, values)
    attended = attended_t.T
    resid_mid = (
        resid_in[0].astype(jnp.float32) + jnp.dot(attended, w_o, preferred_element_type=jnp.float32)
    ).astype(jnp.bfloat16)
    resid_f = resid_mid.astype(jnp.float32)
    inverse_rms = lax.rsqrt(jnp.mean(resid_f * resid_f, axis=-1, keepdims=True) + EPSILON)
    normed = resid_f * inverse_rms
    normed_bf = normed.astype(jnp.bfloat16)
    projected = jnp.dot(normed_bf, w_b, preferred_element_type=jnp.float32).astype(jnp.bfloat16)
    query_b = projected[:, : H * DH]
    key_b = projected[:, H * DH : H * DH + KV * DH]
    value_b = projected[:, H * DH + KV * DH :]
    tails = from_behind(projected[:, H * DH :], "ctx", 1)
    tail_keys, tail_values = (tails[:, : KV * DH], tails[:, KV * DH :])
    keys_ext = jnp.concatenate([tail_keys, key_b], axis=0)
    values_ext = jnp.concatenate([tail_values, value_b], axis=0)
    doc_pad = jnp.concatenate([jnp.full((band_len,), -1, jnp.int32), documents])
    doc_ext = lax.dynamic_slice_in_dim(doc_pad, first_row, band_len + local_rows)
    ext_places = first_row - band_len + jnp.arange(band_len + local_rows, dtype=jnp.int32)
    ext_places = ext_places[:, None]
    band_t = (doc_ext[:, None] == row_docs) & (ext_places <= row_places)
    band_t = (band_t & (ext_places > row_places - band_len)).astype(jnp.float32)
    banded_t, grad_qb_t, key_heads, value_heads = attend(
        band_t, query_b.T, keys_ext, values_ext, None, grad_out[0].T
    )
    banded, grad_qb = (banded_t.T, grad_qb_t.T)
    key_ext_grad, value_ext_grad = (from_heads(key_heads), from_heads(value_heads))
    heads = jnp.concatenate([key_ext_grad[:band_len], value_ext_grad[:band_len]], axis=1)
    heads = from_behind(heads.astype(jnp.bfloat16), "ctx", -1).astype(jnp.float32)
    head_keys, head_values = (heads[:, : KV * DH], heads[:, KV * DH :])
    grad_kb = key_ext_grad[band_len:].at[local_rows - band_len :].add(head_keys)
    grad_vb = value_ext_grad[band_len:].at[local_rows - band_len :].add(head_values)
    grad_kb = (grad_kb * DH ** (-0.5)).astype(jnp.bfloat16)
    grad_vb = grad_vb.astype(jnp.bfloat16)
    grad_proj = jnp.concatenate([grad_qb, grad_kb, grad_vb], axis=1)
    grad_normed = jnp.dot(grad_proj, w_b.T, preferred_element_type=jnp.float32)
    middle = jnp.mean(grad_normed * normed, axis=-1, keepdims=True)
    grad_mid = (
        grad_resid[0].astype(jnp.float32) + inverse_rms * (grad_normed - normed * middle)
    ).astype(jnp.bfloat16)
    grad_attended = jnp.dot(grad_mid, w_o.T, preferred_element_type=jnp.float32).astype(
        jnp.bfloat16
    )
    grad_query_t, key_heads, value_heads = attend(
        allowed_t, query_t, keys, values, attended_t, grad_attended.T
    )
    grad_query = grad_query_t.T
    key_sums, value_sums = (from_heads(key_heads), from_heads(value_heads))
    if own_kernels:
        norm_t = normed_bf.T.reshape(fsdp_count, -1, local_rows)
        kv_sums = jnp.concatenate([key_sums, value_sums], axis=1).astype(jnp.bfloat16)
        out_share, qkv_share, own_kv = reduce_weights(
            attended_t, norm_t, grad_mid, grad_proj, kv_sums
        )
        own_keys, own_values = (own_kv[:, : KV * DH], own_kv[:, KV * DH :])
        grad_w_out, grad_w_qkv = (out_share.astype(jnp.float32), qkv_share.astype(jnp.float32))
    else:
        own_keys, own_values = (
            lax.psum_scatter(
                key_sums.astype(jnp.bfloat16), "ctx", scatter_dimension=0, tiled=True
            ).astype(jnp.float32),
            lax.psum_scatter(
                value_sums.astype(jnp.bfloat16), "ctx", scatter_dimension=0, tiled=True
            ).astype(jnp.float32),
        )
        piece = normed_bf
        qkv_share = lax.psum_scatter(
            jnp.einsum("tf,tc->fc", piece, grad_proj, preferred_element_type=jnp.float32).astype(
                jnp.bfloat16
            ),
            "fsdp",
            scatter_dimension=0,
            tiled=True,
        )
        piece = attended
        out_share = lax.psum_scatter(
            jnp.einsum("tf,tc->fc", piece, grad_mid, preferred_element_type=jnp.float32).astype(
                jnp.bfloat16
            ),
            "fsdp",
            scatter_dimension=0,
            tiled=True,
        )
        grad_w_out, grad_w_qkv = (
            lax.psum(out_share, "ctx").astype(jnp.float32),
            lax.psum(qkv_share, "ctx").astype(jnp.float32),
        )
    grad_key = (own_keys * DH ** (-0.5)).astype(jnp.bfloat16)
    grad_value = own_values.astype(jnp.bfloat16)
    return (
        banded[None],
        grad_mid[None],
        grad_query[None],
        grad_key[None],
        grad_value[None],
        grad_w_out,
        grad_w_qkv,
    )


def solution(mesh):
    in_specs = (
        P("fsdp", "ctx", None),
        P("fsdp", "ctx", None),
        P("fsdp", "ctx", None),
        P("fsdp", "ctx", None),
        P("fsdp", None),
        P("fsdp", None),
        P("fsdp", None),
        P("fsdp", "ctx", None),
        P("fsdp", "ctx", None),
    )
    out_specs = (
        P("fsdp", "ctx", None),
        P("fsdp", "ctx", None),
        P("fsdp", "ctx", None),
        P("fsdp", "ctx", None),
        P("fsdp", "ctx", None),
        P("fsdp", None),
        P("fsdp", None),
    )
    return jax.shard_map(
        per_device, mesh=mesh, in_specs=in_specs, out_specs=out_specs, check_vma=False
    )
```

profile of v0, /device:TPU:0, one launch (start us, length us, event | category | flops | bytes accessed | tf_op | source)
XLA Modules:
  0.0 284.3 jit_solution(1404726211749528346)
XLA Ops:
  2.1 2.3 copy.78.wo
  4.3 1.5 pad_maximum_fusion.2.kv
  5.9 67.9 %shard_map.154 = (bf16[8,256,1440]{2,1,0:T(8,128)(2,1)}, bf16[8,180,2560]{2,1,0:T(8,128)(2,1)}, bf16[512,512]{1,0:T(8,128)(2,1)}) custom-call(bf16[256,1440]{1,0:T(8,128)(2,1)} %copy.78.wo, bf16[180,2560]{1,0:T(8,128)(2,1)} %wq.1, bf16[128,512]{1,0:T(8,128)(2,1)} %pad_maximum_fusion.2.kv), custom_call_target="tpu_custom_call" | custom-call | tf_op jit(solution)/shard_map/pallas_call | solution.py:273
  73.8 7.1 %reshape.163 = bf16[1440,2560]{1,0:T(8,128)(2,1)} reshape(bf16[8,180,2560]{2,1,0:T(8,128)(2,1)} %get-tuple-element.62) | data formatting | bytes 14745600 | tf_op jit(solution)/shard_map/reshape | solution.py:515
  83.0 2.1 slice_bitcast_fusion.2
  85.1 2.0 copy.80
  88.1 1.9 copy.76
  90.9 13.5 %shard_map.155.refs_7_.att_t = bf16[2048,128]{1,0:T(8,128)(2,1)} custom-call(f32[512,128]{1,0:T(8,128)} %fusion.4.refs_0_, bf16[2048,128]{1,0:T(8,128)(2,1)} %bitcast.76, bf16[4,512,64]{2,1,0:T(8,128)(2,1)} %bitcast.78, bf16[4,512,64]{2,1,0:T(8,128)(2,1)} %bitcast.80, bf16[256,512]{1,0:T(8,128)(2,1)} %get-tuple-element.99.refs_4_), custom_call_target="tpu_custom_call" | custom-call | tf_op jit(solution)/shard_map/pallas_call | solution.py:113
  104.4 4.2 %multiply_reduce_fusion.1 = (f32[128]{0:T(128)S(1)}, f32[128,1440]{1,0:T(8,128)S(1)}) fusion(bf16[2048,128]{1,0:T(8,128)(2,1)} %shard_map.155.refs_7_.att_t, bf16[2048,1440]{1,0:T(8,128)(2,1)} %bitcast.69, bf16[1,128,1440]{2,1,0:T(8,128)(2,1)} %copy.76), kind=kOutput, calls=%fused_computation.8 | convolution fusion | flops 756080512 | bytes 7528960 | tf_op jit(solution)/shard_map/dot_general | solution.py:534
  108.7 3.2 %convolution_convert_fusion = bf16[128,2560]{0,1:T(8,128)(2,1)S(1)} fusion(bf16[1440,2560]{1,0:T(8,128)(2,1)S(1)} %bitcast.68, f32[128,1440]{1,0:T(8,128)S(1)} %get-tuple-element.111, f32[128]{0:T(128)S(1)} %add_rsqrt_fusion), kind=kOutput, calls=%fused_computation | convolution fusion | flops 944414720 | bytes 8765952 | tf_op jit(solution)/shard_map/dot_general | solution.py:540
  114.1 2.0 copy.87
  116.2 1.5 and_convert_fusion.refs_0_
  120.8 17.5 %shard_map.156 = (bf16[2048,128]{1,0:T(8,128)(2,1)}, bf16[2048,128]{1,0:T(8,128)(2,1)}, f32[4,256,64]{2,1,0:T(8,128)}, f32[4,256,64]{2,1,0:T(8,128)}) custom-call(f32[256,128]{1,0:T(8,128)} %and_convert_fusion.refs_0_, bf16[2048,128]{1,0:T(8,128)(2,1)} %slice_bitcast_fusion.refs_1_, bf16[4,256,64]{2,1,0:T(8,128)(2,1)} %bitcast.83, ...), custom_call_target="tpu_custom_call" | custom-call | tf_op jit(solution)/shard_map/pallas_call | solution.py:113
  140.6 1.5 collective-permute-start.1
  144.3 2.0 copy.105
  148.4 5.7 %fusion.13 = f32[128,1440]{1,0:T(8,128)S(1)} fusion(bf16[1440,2560]{1,0:T(8,128)(2,1)} %reshape.163, bf16[128,256]{1,0:T(8,128)(2,1)S(1)} %get-tuple-element.103, bf16[128,256]{1,0:T(8,128)(2,1)S(1)} %get-tuple-element.102, bf16[128,2048]{1,0:T(8,128)(2,1)S(1)} %bitcast.74), kind=kOutput, calls=%fused_computation.47 | convolution fusion | flops 945684480 | bytes 8765440 | tf_op jit(solution)/shard_map/dot_general | solution.py:567
  155.6 2.6 convolution_convert_fusion.1.refs_6_
  159.2 17.0 %shard_map.157 = (bf16[2048,128]{1,0:T(8,128)(2,1)}, f32[4,512,64]{2,1,0:T(8,128)}, f32[4,512,64]{2,1,0:T(8,128)}) custom-call(f32[512,128]{1,0:T(8,128)} %fusion.4.refs_0_, bf16[2048,128]{1,0:T(8,128)(2,1)} %bitcast.77, bf16[4,512,64]{2,1,0:T(8,128)(2,1)} %bitcast.79, bf16[4,512,64]{2,1,0:T(8,128)(2,1)} %bitcast.81, ...), custom_call_target="tpu_custom_call" | custom-call | tf_op jit(solution)/shard_map/pallas_call | solution.py:113
  176.2 1.4 convert_bitcast_fusion
  180.4 93.8 %shard_map.158 = (bf16[256,1440]{1,0:T(8,128)(2,1)}, bf16[180,2560]{1,0:T(8,128)(2,1)}, f32[128,512]{1,0:T(8,128)}) custom-call(bf16[2048,128]{1,0:T(8,128)(2,1)} %shard_map.155.refs_7_.att_t, bf16[8,180,128]{2,1,0:T(8,128)(2,1)} %reshape.166.norm_t, bf16[128,1440]{1,0:T(8,128)(2,1)} %copy-done.2, bf16[128,2560]{1,0:T(8,128)(2,1)} %pad_maximum_fusion.grad_proj, ...), custom_call_target="tpu_custom_call" | custom-call | tf_op jit(solution)/shard_map/pallas_call | solution.py:475
  274.1 1.5 fusion.8
  275.7 1.5 fusion.9
  279.2 2.5 copy.108
  281.7 2.6 convert_element_type.79
  (82 shorter events, 24.4 us)
Async XLA Ops:
  1.2 88.9 %copy-start.8 = (s32[128]{0:T(128)}, s32[128]{0:T(128)S(1)}, u32[]{:S(2)}) copy-start(s32[128]{0:T(128)S(1)} %get-tuple-element.112) | copy-start | bytes 1540
  73.8 7.1 %copy-start.4 = (bf16[1,128,2048]{2,1,0:T(8,128)(2,1)S(1)}, bf16[1,128,2048]{2,1,0:T(8,128)(2,1)}, u32[]{:S(2)}) copy-start(bf16[1,128,2048]{2,1,0:T(8,128)(2,1)} %param.17) | copy-start | bytes 1572868
  73.8 8.1 %copy-start.6 = (bf16[512,512]{1,0:T(8,128)(2,1)S(1)}, bf16[512,512]{1,0:T(8,128)(2,1)}, u32[]{:S(2)}) copy-start(bf16[512,512]{1,0:T(8,128)(2,1)} %get-tuple-element.60) | copy-start | bytes 1572868
  83.0 25.7 %slice-start = ((s8[7372800]{0:T(1024)(128)(4,1)}), s8[3178496]{0:T(1024)(128)(4,1)S(1)}, s32[]{:S(2)}) async-start(s8[7372800]{0:T(1024)(128)(4,1)} %bitcast.67), calls=%async_computation | async-start | bytes 6356992
  90.0 18.6 %copy-start.9 = (s32[128]{0:T(128)}, s32[128]{0:T(128)S(1)}, u32[]{:S(2)}) copy-start(s32[128]{0:T(128)S(1)} %dynamic_slice.7) | copy-start | bytes 1540
  104.4 4.3 %slice-start.1 = ((s8[7372800]{0:T(1024)(128)(4,1)}), s8[4194304]{0:T(1024)(128)(4,1)S(1)}, s32[]{:S(2)}) async-start(s8[7372800]{0:T(1024)(128)(4,1)} %bitcast.67), calls=%async_computation.1 | async-start | bytes 8388608
  108.6 3.3 %copy-start = (f32[128,1440]{1,0:T(8,128)}, f32[128,1440]{1,0:T(8,128)S(1)}, u32[]{:S(2)}) copy-start(f32[128,1440]{1,0:T(8,128)S(1)} %get-tuple-element.111) | copy-start | bytes 2211844
  108.7 33.4 %copy-start.7 = (bf16[1,128,1440]{1,2,0:T(8,128)(2,1)S(1)}, bf16[1,128,1440]{1,2,0:T(8,128)(2,1)}, u32[]{:S(2)}) copy-start(bf16[1,128,1440]{1,2,0:T(8,128)(2,1)} %param.25) | copy-start | bytes 1105924
  111.9 5.8 %collective-permute-start = (bf16[128,512]{0,1:T(8,128)(2,1)S(1)}, bf16[128,512]{0,1:T(8,128)(2,1)S(1)}, u32[]{:S(2)}, u32[]{:S(2)}) collective-permute-start(bf16[128,512]{0,1:T(8,128)(2,1)S(1)} %slice.114), channel_id=1, source_target_pairs={{0,8},{8,16},{16,24},{1,9},{9,17},{17,25},{2,10},{10,18},{18,26},{... | collective-permute-start | bytes 393224 | tf_op jit(solution)/shard_map/ppermute | solution.py:23
  140.6 7.7 %collective-permute-start.1 = (bf16[128,512]{1,0:T(8,128)(2,1)S(1)}, bf16[128,512]{1,0:T(8,128)(2,1)S(1)}, u32[]{:S(2)}, u32[]{:S(2)}) collective-permute-start(bf16[128,512]{1,0:T(8,128)(2,1)S(1)} %pad_maximum_fusion.5), channel_id=1, source_target_pairs={{8,0},{16,8},{24,16},{9,1},{17,9},{25,17},{10,2},{18,10},{26,18},{... | collective-permute-start | bytes 393224 | tf_op jit(solution)/shard_map/ppermute | solution.py:23
  146.7 8.3 %copy-start.1 = (f32[128,1440]{1,0:T(8,128)S(1)}, f32[128,1440]{1,0:T(8,128)}, u32[]{:S(2)}) copy-start(f32[128,1440]{1,0:T(8,128)} %copy-done) | copy-start | bytes 2211844
  148.4 7.1 %slice-start.2 = ((s8[6291456]{0:T(1024)(128)(4,1)}), s8[4194304]{0:T(1024)(128)(4,1)S(1)}, s32[]{:S(2)}) async-start(s8[6291456]{0:T(1024)(128)(4,1)} %bitcast.70), calls=%async_computation.2 | async-start | bytes 8388608
  148.4 7.1 %slice-start.3 = ((s8[6291456]{0:T(1024)(128)(4,1)}), s8[2097152]{0:T(1024)(128)(4,1)S(1)}, s32[]{:S(2)}) async-start(s8[6291456]{0:T(1024)(128)(4,1)} %bitcast.70), calls=%async_computation.3 | async-start | bytes 4194304
  155.6 3.7 %copy-start.2 = (bf16[128,1440]{1,0:T(8,128)(2,1)}, bf16[128,1440]{1,0:T(8,128)(2,1)S(1)}, u32[]{:S(2)}) copy-start(bf16[128,1440]{1,0:T(8,128)(2,1)S(1)} %fusion.2.grad_mid) | copy-start | bytes 1105924
  159.2 118.0 %copy-start.3 = (bf16[128,1440]{1,0:T(8,128)(2,1)S(1)}, bf16[128,1440]{1,0:T(8,128)(2,1)}, u32[]{:S(2)}) copy-start(bf16[128,1440]{1,0:T(8,128)(2,1)} %copy-done.2) | copy-start | bytes 1105924
  176.2 101.9 %copy-start.5 = (bf16[2048,128]{1,0:T(8,128)(2,1)S(1)}, bf16[2048,128]{1,0:T(8,128)(2,1)}, u32[]{:S(2)}) copy-start(bf16[2048,128]{1,0:T(8,128)(2,1)} %get-tuple-element.67) | copy-start | bytes 1572868
where the time goes:
time: 285 us; the launch traced here: 284 us
  Pallas kernels  210 us (74%)
  local copies, waits for them, and re-layouts  39 us (14%)
  other arithmetic  15.9 us (6%)
  matrix products  15.7 us (6%)
    pallas_call x1, Pallas kernels, reduce_weights(): pl.pallas_call(functools.partial(reduce_kernel, planes), out_shape=(jax.S...  93.8 us
    pallas_call x1, Pallas kernels, gather_weights(): pl.pallas_call(functools.partial(gather_kernel, planes), out_shape=(jax.S...  67.9 us
    pallas_call x3, Pallas kernels, attend(): pl.pallas_call(functools.partial(attend_kernel, with_output, with_grads),...  48 us
    unnamed x37, local copies, waits for them, and re-layouts  14 us
    reshape x1, local copies, waits for them, and re-layouts, per_device(): w_b = w_b3.reshape(-1, w_qkv.shape[1])  7.11 us
  transfers between devices with their start and end apart: 2, of which 1 were waited for; matrix products, arithmetic and copies ran while one was open for 4% of the time, Pallas kernels for 0%

commit v1 on v0

--- a/solution.py
+++ b/solution.py
@@ -497,6 +497,620 @@
     )(att_t, norm_t, grad_mid, grad_proj, kv_sums)
 
 
+def mega_kernel(
+    planes,
+    lens,
+    q_in,
+    k_in,
+    v_in,
+    resid_in,
+    wo_in,
+    wq_in,
+    go_in,
+    gr_in,
+    out_b,
+    out_gm,
+    out_dq,
+    out_dk,
+    out_dv,
+    res_o,
+    res_q,
+    q_v,
+    resid_v,
+    wo_v,
+    go_v,
+    gr_v,
+    w_o,
+    w_q,
+    kv,
+    kh,
+    vh,
+    kv_t,
+    qp,
+    gp,
+    bias,
+    bias_b,
+    probs,
+    o_p,
+    att_t,
+    att8,
+    attq,
+    acc,
+    acc_p,
+    normed,
+    inv,
+    xb,
+    nt,
+    kvx,
+    khb,
+    vhb,
+    kvx_t,
+    qb,
+    ob_t,
+    dqb_t,
+    dkv_b,
+    tail,
+    head,
+    gp4,
+    gpq,
+    gn,
+    gm,
+    dkv_t,
+    kvs,
+    kvr,
+    s_q,
+    p_q,
+    z_q,
+    t_q,
+    s_o,
+    p_o,
+    z_o,
+    t_o,
+    local,
+    send,
+    recv_kv,
+    recv_z,
+    recv_x,
+    recv_y,
+    recv_d,
+    recv_p,
+    recv_att,
+    recv_nt,
+    recv_halo,
+    recv_gp,
+    recv_gm,
+    recv_kvs,
+    recv_rp,
+    recv_rz,
+    recv_f,
+):
+    f32, bf = (jnp.float32, jnp.bfloat16)
+    c, f = place()
+    z, core = (f // 2, lax.rem(f, 2))
+    toks = q_in.shape[0]
+    kvd = k_in.shape[1]
+    shards = 2 * planes
+    groups = kh.shape[0]
+    pairs = qp.shape[0]
+    per_group = pairs // groups
+    per_shard = att_t.shape[1]
+    scale = DH ** (-0.5)
+    full = (w_o, w_q)
+    by_last = (((1,), (1,)), ((), ()))
+    started = []
+
+    def push(*args):
+        copy = remote(*args)
+        copy.start()
+        started.append(copy)
+
+    def arrive(ref, sem):
+        remote(ref, ref, send, sem, c ^ 1, f).wait_recv()
+
+    def dot(a, b):
+        return jnp.dot(a, b, preferred_element_type=f32)
+
+    def dot_nt(a, b):
+        return lax.dot_general(a, b, by_last, preferred_element_type=f32)
+
+    names = ((wo_in, wo_v), (q_in, q_v), (resid_in, resid_v), (go_in, go_v), (gr_in, gr_v))
+    loads = [
+        pltpu.make_async_copy(src, dst, local.at[i]) for i, (src, dst) in enumerate(names)
+    ]
+    loads.append(pltpu.make_async_copy(k_in, kv.at[c, :, pl.ds(0, kvd)], local.at[5]))
+    loads.append(pltpu.make_async_copy(v_in, kv.at[c, :, pl.ds(kvd, kvd)], local.at[6]))
+    loads.append(pltpu.make_async_copy(wq_in, w_q.at[f], local.at[7]))
+    for copy in loads:
+        copy.start()
+    greet(planes)
+    for slot in (1, 2, 3):
+        for i, src in enumerate((k_in, v_in)):
+            push(
+                src,
+                kv.at[c, :, pl.ds(i * kvd, kvd)],
+                send,
+                recv_kv.at[slot, i],
+                c ^ slot,
+                f,
+            )
+    loads[0].wait()
+    w_o[f] = wo_v[...].T
+    order = by_distance(planes)
+
+    def piece(weight, shard, quarter):
+        return quarter_of(full[weight].at[shard], weight, quarter)
+
+    for weight in (0, 1):
+        for d in order:
+            part = piece(0, f, c) if weight == 0 else quarter_of(wq_in, 1, c)
+            push(
+                part,
+                piece(weight, f, c),
+                send,
+                recv_z.at[weight, d],
+                c,
+                shard_at(z, core, planes, d),
+            )
+        push(
+            full[0].at[f] if weight == 0 else wq_in,
+            full[weight].at[f],
+            send,
+            recv_p.at[weight, 0, 0],
+            c,
+            f ^ 1,
+        )
+    steps = [(weight, d) for weight in (0, 1) for d in order]
+    count = len(steps)
+
+    def to_partner(weight, d, shard, slot):
+        part = piece(weight, shard, c ^ slot)
+        push(part, part, send, recv_p.at[weight, d, slot], c, f ^ 1)
+
+    def first(weight, d):
+        shard = shard_at(z, core, planes, planes - d)
+        part = piece(weight, shard, c)
+        arrive(part, recv_z.at[weight, d])
+        push(part, part, send, recv_x.at[weight, d], c ^ 1, f)
+        push(part, part, send, recv_y.at[weight, d], c ^ 2, f)
+        to_partner(weight, d, shard, 0)
+
+    def second(weight, d):
+        shard = shard_at(z, core, planes, planes - d)
+        arrive(piece(weight, shard, c ^ 1), recv_x.at[weight, d])
+        arrive(piece(weight, shard, c ^ 2), recv_y.at[weight, d])
+        bit = jnp.where(core == weight, 1, 2)
+        part = piece(weight, shard, c ^ bit)
+        push(part, part, send, recv_d.at[weight, d], c ^ (3 - bit), f)
+        to_partner(weight, d, shard, 1)
+        to_partner(weight, d, shard, 2)
+
+    def third(weight, d):
+        shard = shard_at(z, core, planes, planes - d)
+        arrive(piece(weight, shard, c ^ 3), recv_d.at[weight, d])
+        to_partner(weight, d, shard, 3)
+
+    def whole_plane(weight, d):
+        shard = shard_at(z, core, planes, planes - d) ^ 1
+        for slot in range(4):
+            arrive(piece(weight, shard, c ^ slot), recv_p.at[weight, d, slot])
+
+    def gather_step(i):
+        if i < count:
+            first(*steps[i])
+        if 0 <= i - 1 < count:
+            second(*steps[i - 1])
+        if 0 <= i - 2 < count:
+            third(*steps[i - 2])
+
+    ends = [lens[0, 0]]
+    for i in range(1, lens.shape[1]):
+        ends.append(ends[-1] + lens[0, i])
+
+    def document(places):
+        number = jnp.zeros(places.shape, jnp.int32)
+        for end in ends:
+            number = number + (places >= end).astype(jnp.int32)
+        return number
+
+    def bias_of(length, first_place, reach):
+        shape = (length, toks)
+        columns = lax.broadcasted_iota(jnp.int32, shape, 0) + first_place
+        rows = lax.broadcasted_iota(jnp.int32, shape, 1) + c * toks
+        allowed = (document(columns) == document(rows)) & (columns <= rows)
+        if reach:
+            allowed = allowed & (columns > rows - reach) & (columns >= 0)
+        part = jnp.where(allowed, 0.0, MASKED).astype(f32)
+        return jnp.concatenate([part, part], axis=1)
+
+    bias[...] = bias_of(kv.shape[0] * toks, 0, 0)
+    bias_b[...] = bias_of(2 * toks, (c - 1) * toks, BAND)
+
+    def paired(tile):
+        return jnp.concatenate([tile[:DH], tile[DH:]], axis=1)
+
+    def unpaired(wide):
+        return jnp.concatenate([wide[:, :toks], wide[:, toks:]], axis=0)
+
+    wide = 2 * DH
+
+    def scaled(tile):
+        return (tile.astype(f32) * scale).astype(bf)
+
+    loads[1].wait()
+    for i in range(pairs):
+        qp[i] = scaled(paired(q_v[:, wide * i : wide * (i + 1)].T))
+    for copy in loads[5:7]:
+        copy.wait()
+    for slot in (1, 2, 3):
+        for i in range(2):
+            arrive(kv.at[c ^ slot, :, pl.ds(i * kvd, kvd)], recv_kv.at[slot, i])
+
+    def spread(source, keys_to, values_to, both_t):
+        both = source[...].reshape(-1, 2 * kvd)
+        for g in range(groups):
+            keys_to[g] = both[:, DH * g : DH * (g + 1)]
+            values_to[g] = both[:, kvd + DH * g : kvd + DH * (g + 1)]
+        turned = both.T
+        for g in range(2 * groups):
+            both_t[g] = turned[DH * g : DH * (g + 1)]
+
+    spread(kv, kh, vh, kv_t)
+
+    def softmax(scores):
+        top = jnp.max(scores, axis=0, keepdims=True)
+        raised = jnp.exp(scores - top)
+        total = jnp.sum(raised, axis=0, keepdims=True)
+        return raised * (1.0 / total)
+
+    def forward(g):
+        for j in range(per_group):
+            i = per_group * g + j
+            weights = softmax(dot(kh[g], qp[i]) + bias[...]).astype(bf)
+            probs[i] = weights
+            output = dot(kv_t[groups + g], weights).astype(bf)
+            o_p[i] = output
+            att_t[i // per_shard, i % per_shard] = unpaired(output)
+
+    for g in range(groups):
+        forward(g)
+        gather_step(g)
+    for slot in (1, 2, 3):
+        peer = c ^ slot
+        push(
+            att_t.at[:, peer // 2, pl.ds(pl.multiple_of(lax.rem(peer, 2) * DH, DH), DH), :],
+            attq.at[c],
+            send,
+            recv_att.at[slot],
+            peer,
+            f,
+        )
+    attq[c] = att_t[:, c // 2, pl.ds(pl.multiple_of(lax.rem(c, 2) * DH, DH), DH), :]
+    for s in range(shards):
+        for j in range(per_shard):
+            att8[s, :, wide * j : wide * (j + 1)] = att_t[s, j].T
+    loads[2].wait()
+    loads[3].wait()
+    loads[4].wait()
+    acc[...] = resid_v[...].astype(f32).T
+    for i in range(pairs):
+        gp[i] = paired(go_v[:, wide * i : wide * (i + 1)].T)
+
+    def project(weight, shard):
+        left = (att8, xb)[weight]
+        return dot(left[shard], full[weight][shard]) + dot(left[shard ^ 1], full[weight][shard ^ 1])
+
+    arrive(w_o.at[f ^ 1], recv_p.at[0, 0, 0])
+    acc[...] += project(0, f)
+    at = groups
+    for d in order:
+        gather_step(at)
+        at += 1
+        whole_plane(0, d)
+        acc[...] += project(0, shard_at(z, core, planes, planes - d))
+    resid = acc[...].astype(bf).astype(f32)
+    inverse = lax.rsqrt(jnp.mean(resid * resid, axis=1, keepdims=True) + EPSILON)
+    inv[...] = inverse
+    values = resid * inverse
+    normed[...] = values
+    rows_q = w_q.shape[1]
+    for s in range(shards):
+        xb[s] = values[:, rows_q * s : rows_q * (s + 1)].astype(bf)
+    loads[7].wait()
+    arrive(w_q.at[f ^ 1], recv_p.at[1, 0, 0])
+    acc_p[...] = project(1, f)
+    for s in range(shards):
+        nt[c, s] = xb[s].T
+    for slot in (1, 2, 3):
+        push(nt.at[c], nt.at[c], send, recv_nt.at[slot], c ^ slot, f)
+    for d in order:
+        if at < count + 2:
+            gather_step(at)
+            at += 1
+        whole_plane(1, d)
+        acc_p[...] += project(1, shard_at(z, core, planes, planes - d))
+
+    width = qb.shape[0] * wide
+    kvx[1] = acc_p[:, width:].astype(bf)
+    ahead, behind = (lax.rem(c + 1, 4), lax.rem(c + 3, 4))
+    push(kvx.at[1], kvx.at[0], send, recv_halo.at[0], ahead, f)
+    for i in range(pairs):
+        qb[i] = scaled(paired(acc_p[:, wide * i : wide * (i + 1)].astype(bf).T))
+    arrive(kvx.at[0], recv_halo.at[0])
+    spread(kvx, khb, vhb, kvx_t)
+
+    def banded(g, carry):
+        dk = jnp.zeros((DH, 2 * toks), f32)
+        dv = jnp.zeros((DH, 2 * toks), f32)
+        for j in range(per_group):
+            i = per_group * g + j
+            weights = softmax(dot(khb[g], qb[i]) + bias_b[...])
+            weights_bf = weights.astype(bf)
+            output = dot(kvx_t[groups + g], weights_bf).astype(bf)
+            ob_t[i] = unpaired(output)
+            grad = gp[i]
+            correction = jnp.sum(grad.astype(f32) * output.astype(f32), axis=0, keepdims=True)
+            grad_scores = (weights * (dot(vhb[g], grad) - correction)).astype(bf)
+            dqb_t[i] = unpaired((dot(kvx_t[g], grad_scores) * scale).astype(bf))
+            dk += dot_nt(qb[i], grad_scores)
+            dv += dot_nt(grad, weights_bf)
+        dkv_b[g] = dk
+        dkv_b[groups + g] = dv
+        return carry
+
+    lax.fori_loop(0, groups, banded, 0)
+    for g in range(2 * groups):
+        tail[DH * g : DH * (g + 1)] = dkv_b[g, :, :toks].astype(bf)
+    push(tail, head, send, recv_halo.at[1], behind, f)
+    gp_width = gp4.shape[2]
+
+    def put_gp(column, block):
+        gp4[column // gp_width, :, column % gp_width : column % gp_width + block.shape[1]] = block
+
+    for i in range(pairs):
+        out_b[:, wide * i : wide * (i + 1)] = ob_t[i].T
+        put_gp(wide * i, dqb_t[i].T)
+    arrive(head, recv_halo.at[1])
+    own = jnp.concatenate([dkv_b[g, :, toks:] for g in range(2 * groups)], axis=0)
+    own = (own + head[...].astype(f32)).astype(bf)
+    for i in range(2 * groups * DH // wide):
+        put_gp(width + wide * i, own[wide * i : wide * (i + 1)].T)
+    for slot in (1, 2, 3):
+        push(gp4.at[c ^ slot], gpq.at[c], send, recv_gp.at[slot], c ^ slot, f)
+    gpq[c] = gp4[c]
+
+    for s in range(shards):
+        total = dot_nt(gp4[0], w_q[s, :, :gp_width])
+        for b in range(1, 4):
+            total += dot_nt(gp4[b], w_q[s, :, gp_width * b : gp_width * (b + 1)])
+        gn[:, rows_q * s : rows_q * (s + 1)] = total
+    middle = jnp.mean(gn[...] * normed[...], axis=1, keepdims=True)
+    change = inv[...] * (gn[...] - normed[...] * middle)
+    grad_mid = gr_v[...].astype(f32).T + change
+    gm[c] = grad_mid.astype(bf)
+    for slot in (1, 2, 3):
+        push(gm.at[c], gm.at[c], send, recv_gm.at[slot], c ^ slot, f)
+    out_gm[...] = gm[c].T
+
+    def sum_parts(weight, produce, sent, from_p, from_z, total):
+        for d in order[::-1] + [0]:
+            sent[d] = produce(shard_at(z, 1 - core, planes, d)).astype(bf)
+            push(sent.at[d], from_p.at[d], send, recv_rp.at[weight, d], c, f ^ 1)
+        for d in order[::-1] + [0]:
+            mine = produce(shard_at(z, core, planes, d))
+            arrive(from_p.at[d], recv_rp.at[weight, d])
+            mine = mine + from_p[d].astype(f32)
+            if d:
+                from_z[planes + d] = mine.astype(bf)
+                push(
+                    from_z.at[planes + d],
+                    from_z.at[d],
+                    send,
+                    recv_rz.at[weight, d],
+                    c,
+                    shard_at(z, core, planes, d),
+                )
+            else:
+                total[...] = mine
+
+    def finish(weight, from_z, total, result):
+        value = total[...]
+        for d in range(1, planes):
+            arrive(from_z.at[d], recv_rz.at[weight, d])
+            value = value + from_z[d].astype(f32)
+        result[c] = value.astype(bf)
+        for slot in (3, 1, 2):
+            push(result.at[c], result.at[c], send, recv_f.at[weight, slot], c ^ slot, f)
+
+    def produce_q(shard):
+        left = jnp.concatenate([nt[b, shard] for b in range(4)], axis=1)
+        return dot(left, gpq[...].reshape(-1, gp_width))
+
+    def produce_o(shard):
+        left = jnp.concatenate([attq[b, shard] for b in range(4)], axis=1)
+        return dot(left, gm[...].reshape(-1, gm.shape[2]))
+
+    for s in range(shards):
+        part = dot(w_o[s], out_gm[...]).astype(bf)
+        for j in range(per_shard):
+            gp[per_shard * s + j] = paired(part[wide * j : wide * (j + 1)])
+    for slot in (1, 2, 3):
+        arrive(nt.at[c ^ slot], recv_nt.at[slot])
+        arrive(gpq.at[c ^ slot], recv_gp.at[slot])
+    sum_parts(1, produce_q, s_q, p_q, z_q, t_q)
+
+    def backward(g, carry):
+        dk = jnp.zeros((DH, 4 * toks), f32)
+        dv = jnp.zeros((DH, 4 * toks), f32)
+        for j in range(per_group):
+            i = per_group * g + j
+            grad, weights = (gp[i], probs[i])
+            correction = jnp.sum(grad.astype(f32) * o_p[i].astype(f32), axis=0, keepdims=True)
+            change = dot(vh[g], grad) - correction
+            grad_scores = (weights.astype(f32) * change).astype(bf)
+            dqb_t[i] = unpaired((dot(kv_t[g], grad_scores) * scale).astype(bf))
+            dk += dot_nt(qp[i], grad_scores)
+            dv += dot_nt(grad, weights)
+        dkv_t[g] = dk
+        dkv_t[groups + g] = dv
+        return carry
+
+    lax.fori_loop(0, groups, backward, 0)
+    for b in range(4):
+        for g in range(2 * groups):
+            kvs[b, DH * g : DH * (g + 1)] = dkv_t[g, :, toks * b : toks * (b + 1)].astype(bf)
+    for slot in (1, 2, 3):
+        push(kvs.at[c ^ slot], kvr.at[slot], send, recv_kvs.at[slot], c ^ slot, f)
+    for slot in (1, 2, 3):
+        arrive(attq.at[c ^ slot], recv_att.at[slot])
+        arrive(gm.at[c ^ slot], recv_gm.at[slot])
+    sum_parts(0, produce_o, s_o, p_o, z_o, t_o)
+    for i in range(pairs):
+        out_dq[:, wide * i : wide * (i + 1)] = dqb_t[i].T
+    finish(1, z_q, t_q, res_q)
+    total = kvs[c].astype(f32)
+    for slot in (1, 2, 3):
+        arrive(kvr.at[slot], recv_kvs.at[slot])
+        total += kvr[slot].astype(f32)
+    total = total.astype(bf).T
+    out_dk[...] = total[:, :kvd]
+    out_dv[...] = total[:, kvd:]
+    finish(0, z_o, t_o, res_o)
+    for weight, result in ((1, res_q), (0, res_o)):
+        for slot in (3, 1, 2):
+            arrive(result.at[c ^ slot], recv_f.at[weight, slot])
+    for copy in started:
+        copy.wait_send()
+
+
+def finish_kernel(b_in, gm_in, dq_in, dk_in, dv_in, o_in, q_in, b, gm, dq, dk, dv, wo, wq):
+    for src, dst in ((b_in, b), (gm_in, gm), (dq_in, dq), (dk_in, dk), (dv_in, dv)):
+        dst[...] = src[...]
+    width = q_in.shape[2]
+    for quarter in range(4):
+        wq[:, width * quarter : width * (quarter + 1)] = q_in[quarter].astype(jnp.float32)
+    whole = o_in[...].reshape(-1, o_in.shape[2]).astype(jnp.float32)
+    wo[...] = whole.T
+
+
+def one_kernel(lengths, query, keys, values, resid, w_out, w_qkv, grad_out, grad_resid):
+    shards = lax.axis_size("fsdp")
+    planes = shards // 2
+    bf, f32 = (jnp.bfloat16, jnp.float32)
+    toks, hd = query.shape
+    kvd = keys.shape[1]
+    dim = resid.shape[1]
+    rows_o, rows_q = (w_out.shape[0], w_qkv.shape[0])
+    width = w_qkv.shape[1]
+    wide = 2 * DH
+    pairs = hd // wide
+    groups = kvd // DH
+    seq = 4 * toks
+    shape = jax.ShapeDtypeStruct
+    o_part, q_part = ((rows_o // 4, dim), (rows_q, width // 4))
+    outs = (
+        shape((toks, hd), bf),
+        shape((dim, toks), bf),
+        shape((toks, hd), bf),
+        shape((toks, kvd), bf),
+        shape((toks, kvd), bf),
+        shape((4,) + o_part, bf),
+        shape((4,) + q_part, bf),
+    )
+    v = pltpu.VMEM
+    scratch = [
+        v((toks, hd), bf),
+        v((dim, toks), bf),
+        v((dim, rows_o), bf),
+        v((toks, hd), bf),
+        v((dim, toks), bf),
+        v((shards, rows_o, dim), bf),
+        v((shards, rows_q, width), bf),
+        v((4, toks, 2 * kvd), bf),
+        v((groups, seq, DH), bf),
+        v((groups, seq, DH), bf),
+        v((2 * groups, DH, seq), bf),
+        v((pairs, DH, 2 * toks), bf),
+        v((pairs, DH, 2 * toks), bf),
+        v((seq, 2 * toks), f32),
+        v((2 * toks, 2 * toks), f32),
+        v((pairs, seq, 2 * toks), bf),
+        v((pairs, DH, 2 * toks), bf),
+        v((shards, rows_o // wide, wide, toks), bf),
+        v((shards, toks, rows_o), bf),
+        v((4, shards, rows_o // 4, toks), bf),
+        v((toks, dim), f32),
+        v((toks, width), f32),
+        v((toks, dim), f32),
+        v((toks, 1), f32),
+        v((shards, toks, rows_q), bf),
+        v((4, shards, rows_q, toks), bf),
+        v((2, toks, 2 * kvd), bf),
+        v((groups, 2 * toks, DH), bf),
+        v((groups, 2 * toks, DH), bf),
+        v((2 * groups, DH, 2 * toks), bf),
+        v((pairs, DH, 2 * toks), bf),
+        v((pairs, wide, toks), bf),
+        v((pairs, wide, toks), bf),
+        v((2 * groups, DH, 2 * toks), f32),
+        v((2 * kvd, toks), bf),
+        v((2 * kvd, toks), bf),
+        v((4, toks, width // 4), bf),
+        v((4, toks, width // 4), bf),
+        v((toks, dim), f32),
+        v((4, toks, dim), bf),
+        v((2 * groups, DH, seq), f32),
+        v((4, 2 * kvd, toks), bf),
+        v((4, 2 * kvd, toks), bf),
+    ]
+    for part in (q_part, o_part):
+        scratch += [
+            v((planes,) + part, bf),
+            v((planes,) + part, bf),
+            v((2 * planes,) + part, bf),
+            v(part, f32),
+        ]
+    dma = pltpu.SemaphoreType.DMA
+    scratch += [
+        dma((8,)),
+        dma,
+        dma((4, 2)),
+        dma((2, planes)),
+        dma((2, planes)),
+        dma((2, planes)),
+        dma((2, planes)),
+        dma((2, planes, 4)),
+        dma((4,)),
+        dma((4,)),
+        dma((2,)),
+        dma((4,)),
+        dma((4,)),
+        dma((4,)),
+        dma((2, planes)),
+        dma((2, planes)),
+        dma((2, 4)),
+    ]
+    anywhere = pl.BlockSpec(memory_space=pl.ANY)
+    in_vmem = pl.BlockSpec(memory_space=pltpu.VMEM)
+    results = pl.pallas_call(
+        functools.partial(mega_kernel, planes),
+        out_shape=outs,
+        in_specs=[pl.BlockSpec(memory_space=pltpu.SMEM)] + [anywhere] * 8,
+        out_specs=(in_vmem,) * 7,
+        scratch_shapes=scratch,
+        compiler_params=pltpu.CompilerParams(
+            collective_id=0, has_side_effects=True, vmem_limit_bytes=60 * 2**20
+        ),
+    )(lengths, query, keys, values, resid.T, w_out.T, w_qkv, grad_out, grad_resid.T)
+    final = outs[:5] + (shape((dim, rows_o), f32), shape((rows_q, width), f32))
+    b, gm, dq, dk, dv, wo, wq = pl.pallas_call(
+        finish_kernel,
+        out_shape=final,
+        in_specs=[in_vmem] * 7,
+        out_specs=(in_vmem,) * 7,
+    )(*results)
+    return (b[None], gm.T[None], dq[None], dk[None], dv[None], wo.T, wq)
+
+
 def per_device(query_a, key_a, value_a, resid_in, doc_lengths, w_out, w_qkv, grad_out, grad_resid):
     ctx_count = lax.axis_size("ctx")
     ctx_index = lax.axis_index("ctx")
@@ -507,6 +1121,18 @@
     documents = doc_table(doc_lengths[0], seq_len)
     fsdp_count = lax.axis_size("fsdp")
     own_kernels = ctx_count == 4 and fsdp_count % 2 == 0 and w_out.shape[0] % 64 == 0
+    if own_kernels and local_rows == BAND and w_out.shape[0] == 4 * DH and fsdp_count == 8:
+        return one_kernel(
+            doc_lengths,
+            query_a[0],
+            key_a[0],
+            value_a[0],
+            resid_in[0],
+            w_out,
+            w_qkv,
+            grad_out[0],
+            grad_resid[0],
+        )
     if own_kernels:
         w_o3, w_b3, kv = gather_weights(
             w_out, w_qkv, jnp.concatenate([key_a[0], value_a[0]], axis=1)

time: 285 us -> 172 us (0.60)
  the two profiles are of different devices: /device:TPU:0 before, /device:TPU:14 now
where the time goes in v1:
time: 172 us; the launch traced here: 171 us
  Pallas kernels  171 us (99%)
    pallas_call x1, Pallas kernels, one_kernel(): pl.pallas_call(functools.partial(mega_kernel, planes), out_shape=outs, in...  166 us
    pallas_call x1, Pallas kernels, one_kernel(): pl.pallas_call(finish_kernel, out_shape=final, in_specs=[in_vmem] * 7, ou...  4.38 us

profile of v1, /device:TPU:14, one launch (start us, length us, event | category | flops | bytes accessed | tf_op | source)
XLA Modules:
  0.0 171.4 jit_solution(8327689978610524402)
XLA Ops:
  0.6 166.4 %shard_map.144 = (bf16[128,2048]{1,0:T(8,128)(2,1)}, bf16[1440,128]{1,0:T(8,128)(2,1)}, bf16[128,2048]{1,0:T(8,128)(2,1)}, bf16[128,256]{1,0:T(8,128)(2,1)}, bf1...) custom-call(s32[1,6]{1,0:T(1,128)} %lens.1, bf16[128,2048]{1,0:T(8,128)(2,1)} %bitcast.20, ...), custom_call_target="tpu_custom_call" | custom-call | tf_op jit(solution)/shard_map/pallas_call | solution.py:1094
  167.0 4.4 %shard_map.145 = (bf16[128,2048]{1,0:T(8,128)(2,1)}, bf16[1440,128]{1,0:T(8,128)(2,1)}, bf16[128,2048]{1,0:T(8,128)(2,1)}, bf16[128,256]{1,0:T(8,128)(2,1)}, bf1...) custom-call(bf16[128,2048]{1,0:T(8,128)(2,1)} %get-tuple-element.21.b_in, ...), custom_call_target="tpu_custom_call" | custom-call | tf_op jit(solution)/shard_map/pallas_call | solution.py:1105

commit v2 on v1

--- a/solution.py
+++ b/solution.py
@@ -560,10 +560,12 @@
     kvr,
     s_q,
     p_q,
+    o_q,
     z_q,
     t_q,
     s_o,
     p_o,
+    o_o,
     z_o,
     t_o,
     local,
@@ -599,10 +601,21 @@
     by_last = (((1,), (1,)), ((), ()))
     started = []
 
-    def push(*args):
+    def push(*args, when=None):
         copy = remote(*args)
-        copy.start()
-        started.append(copy)
+        if when is None:
+            copy.start()
+        else:
+            pl.when(when)(copy.start)
+        started.append((when, copy))
+
+    def by_plane(table):
+        return sum(jnp.where(z == i, entry, 0) for i, entry in enumerate(table))
+
+    near = [sorted((s for s in range(planes) if s != i), key=lambda s: abs(s - i)) for i in range(planes)]
+    sources = [by_plane(column) for column in zip(*near)]
+    targets = sources[::-1]
+    last = planes - 1
 
     def arrive(ref, sem):
         remote(ref, ref, send, sem, c ^ 1, f).wait_recv()
@@ -612,6 +625,22 @@
 
     def dot_nt(a, b):
         return lax.dot_general(a, b, by_last, preferred_element_type=f32)
+
+    def share_rows(ref, sems):
+        for bit in (1, 2):
+            push(ref.at[c], ref.at[c], send, sems.at[bit], c ^ bit, f)
+
+    def relay_rows(ref, sems):
+        half = ref.shape[1] // 2
+        for bit in (1, 2):
+            arrive(ref.at[c ^ bit], sems.at[bit])
+            part = ref.at[c ^ bit, pl.ds((bit - 1) * half, half)]
+            push(part, part, send, sems.at[2 + bit], c ^ (3 - bit), f)
+
+    def far_rows(ref, sems):
+        half = ref.shape[1] // 2
+        for bit in (1, 2):
+            arrive(ref.at[c ^ 3, pl.ds((bit - 1) * half, half)], sems.at[2 + bit])
 
     names = ((wo_in, wo_v), (q_in, q_v), (resid_in, resid_v), (go_in, go_v), (gr_in, gr_v))
     loads = [
@@ -635,47 +664,47 @@
             )
     loads[0].wait()
     w_o[f] = wo_v[...].T
-    order = by_distance(planes)
+    slots = range(planes - 1)
 
     def piece(weight, shard, quarter):
         return quarter_of(full[weight].at[shard], weight, quarter)
 
-    for weight in (0, 1):
-        for d in order:
-            part = piece(0, f, c) if weight == 0 else quarter_of(wq_in, 1, c)
+    def share(weight):
+        mine = w_o.at[f] if weight == 0 else wq_in
+        for plane, ok in ((z + 1, z < last), (z - 1, z > 0)):
             push(
-                part,
+                quarter_of(mine, weight, c),
                 piece(weight, f, c),
                 send,
-                recv_z.at[weight, d],
+                recv_z.at[weight, z],
                 c,
-                shard_at(z, core, planes, d),
+                2 * plane + core,
+                when=ok,
             )
-        push(
-            full[0].at[f] if weight == 0 else wq_in,
-            full[weight].at[f],
-            send,
-            recv_p.at[weight, 0, 0],
-            c,
-            f ^ 1,
-        )
-    steps = [(weight, d) for weight in (0, 1) for d in order]
+        push(mine, full[weight].at[f], send, recv_p.at[weight, 0, 0], c, f ^ 1)
+
+    share(0)
+    steps = [(weight, d) for weight in (0, 1) for d in slots]
     count = len(steps)
 
     def to_partner(weight, d, shard, slot):
         part = piece(weight, shard, c ^ slot)
-        push(part, part, send, recv_p.at[weight, d, slot], c, f ^ 1)
+        push(part, part, send, recv_p.at[weight, d + 1, slot], c, f ^ 1)
 
     def first(weight, d):
-        shard = shard_at(z, core, planes, planes - d)
+        source = sources[d]
+        shard = 2 * source + core
         part = piece(weight, shard, c)
-        arrive(part, recv_z.at[weight, d])
+        arrive(part, recv_z.at[weight, source])
+        onward = jnp.where(source < z, z < last, z > 0)
+        plane = jnp.where(source < z, z + 1, z - 1)
+        push(part, part, send, recv_z.at[weight, source], c, 2 * plane + core, when=onward)
         push(part, part, send, recv_x.at[weight, d], c ^ 1, f)
         push(part, part, send, recv_y.at[weight, d], c ^ 2, f)
         to_partner(weight, d, shard, 0)
 
     def second(weight, d):
-        shard = shard_at(z, core, planes, planes - d)
+        shard = 2 * sources[d] + core
         arrive(piece(weight, shard, c ^ 1), recv_x.at[weight, d])
         arrive(piece(weight, shard, c ^ 2), recv_y.at[weight, d])
         bit = jnp.where(core == weight, 1, 2)
@@ -685,14 +714,14 @@
         to_partner(weight, d, shard, 2)
 
     def third(weight, d):
-        shard = shard_at(z, core, planes, planes - d)
+        shard = 2 * sources[d] + core
         arrive(piece(weight, shard, c ^ 3), recv_d.at[weight, d])
         to_partner(weight, d, shard, 3)
 
     def whole_plane(weight, d):
-        shard = shard_at(z, core, planes, planes - d) ^ 1
+        shard = 2 * sources[d] + 1 - core
         for slot in range(4):
-            arrive(piece(weight, shard, c ^ slot), recv_p.at[weight, d, slot])
+            arrive(piece(weight, shard, c ^ slot), recv_p.at[weight, d + 1, slot])
 
     def gather_step(i):
         if i < count:
@@ -772,18 +801,10 @@
             att_t[i // per_shard, i % per_shard] = unpaired(output)
 
     for g in range(groups):
+        gather_step(g)
+        if g == 1:
+            share(1)
         forward(g)
-        gather_step(g)
-    for slot in (1, 2, 3):
-        peer = c ^ slot
-        push(
-            att_t.at[:, peer // 2, pl.ds(pl.multiple_of(lax.rem(peer, 2) * DH, DH), DH), :],
-            attq.at[c],
-            send,
-            recv_att.at[slot],
-            peer,
-            f,
-        )
     attq[c] = att_t[:, c // 2, pl.ds(pl.multiple_of(lax.rem(c, 2) * DH, DH), DH), :]
     for s in range(shards):
         for j in range(per_shard):
@@ -802,11 +823,11 @@
     arrive(w_o.at[f ^ 1], recv_p.at[0, 0, 0])
     acc[...] += project(0, f)
     at = groups
-    for d in order:
+    for d in slots:
         gather_step(at)
         at += 1
         whole_plane(0, d)
-        acc[...] += project(0, shard_at(z, core, planes, planes - d))
+        acc[...] += project(0, 2 * sources[d] + core)
     resid = acc[...].astype(bf).astype(f32)
     inverse = lax.rsqrt(jnp.mean(resid * resid, axis=1, keepdims=True) + EPSILON)
     inv[...] = inverse
@@ -820,19 +841,18 @@
     acc_p[...] = project(1, f)
     for s in range(shards):
         nt[c, s] = xb[s].T
-    for slot in (1, 2, 3):
-        push(nt.at[c], nt.at[c], send, recv_nt.at[slot], c ^ slot, f)
-    for d in order:
+    for d in slots:
         if at < count + 2:
             gather_step(at)
             at += 1
         whole_plane(1, d)
-        acc_p[...] += project(1, shard_at(z, core, planes, planes - d))
+        acc_p[...] += project(1, 2 * sources[d] + core)
 
     width = qb.shape[0] * wide
     kvx[1] = acc_p[:, width:].astype(bf)
     ahead, behind = (lax.rem(c + 1, 4), lax.rem(c + 3, 4))
     push(kvx.at[1], kvx.at[0], send, recv_halo.at[0], ahead, f)
+    share_rows(nt, recv_nt)
     for i in range(pairs):
         qb[i] = scaled(paired(acc_p[:, wide * i : wide * (i + 1)].astype(bf).T))
     arrive(kvx.at[0], recv_halo.at[0])
@@ -861,6 +881,7 @@
     for g in range(2 * groups):
         tail[DH * g : DH * (g + 1)] = dkv_b[g, :, :toks].astype(bf)
     push(tail, head, send, recv_halo.at[1], behind, f)
+    relay_rows(nt, recv_nt)
     gp_width = gp4.shape[2]
 
     def put_gp(column, block):
@@ -887,37 +908,57 @@
     change = inv[...] * (gn[...] - normed[...] * middle)
     grad_mid = gr_v[...].astype(f32).T + change
     gm[c] = grad_mid.astype(bf)
+    share_rows(gm, recv_gm)
     for slot in (1, 2, 3):
-        push(gm.at[c], gm.at[c], send, recv_gm.at[slot], c ^ slot, f)
+        peer = c ^ slot
+        push(
+            att_t.at[:, peer // 2, pl.ds(pl.multiple_of(lax.rem(peer, 2) * DH, DH), DH), :],
+            attq.at[c],
+            send,
+            recv_att.at[slot],
+            peer,
+            f,
+        )
     out_gm[...] = gm[c].T
 
-    def sum_parts(weight, produce, sent, from_p, from_z, total):
-        for d in order[::-1] + [0]:
-            sent[d] = produce(shard_at(z, 1 - core, planes, d)).astype(bf)
+    def sum_chip(weight, produce, sent, from_p, totals):
+        for d in range(planes):
+            sent[d] = produce(2 * d + 1 - core).astype(bf)
             push(sent.at[d], from_p.at[d], send, recv_rp.at[weight, d], c, f ^ 1)
-        for d in order[::-1] + [0]:
-            mine = produce(shard_at(z, core, planes, d))
+        for d in range(planes):
+            mine = produce(2 * d + core)
             arrive(from_p.at[d], recv_rp.at[weight, d])
-            mine = mine + from_p[d].astype(f32)
-            if d:
-                from_z[planes + d] = mine.astype(bf)
-                push(
-                    from_z.at[planes + d],
-                    from_z.at[d],
-                    send,
-                    recv_rz.at[weight, d],
-                    c,
-                    shard_at(z, core, planes, d),
-                )
-            else:
-                total[...] = mine
-
-    def finish(weight, from_z, total, result):
-        value = total[...]
-        for d in range(1, planes):
-            arrive(from_z.at[d], recv_rz.at[weight, d])
-            value = value + from_z[d].astype(f32)
-        result[c] = value.astype(bf)
+            totals[d] = mine + from_p[d].astype(f32)
+
+    def chain(weight, slot, totals, out, moving):
+        target = targets[slot]
+        way = jnp.where(target > z, 0, 1)
+        plane = jnp.where(target > z, z + 1, z - 1)
+
+        @pl.when(jnp.where(target > z, z > 0, z < last))
+        def _():
+            arrive(moving.at[way, target], recv_rz.at[weight, way, target])
+            totals[target] += moving[way, target].astype(f32)
+
+        out[slot] = totals[target].astype(bf)
+        push(
+            out.at[slot],
+            moving.at[way, target],
+            send,
+            recv_rz.at[weight, way, target],
+            c,
+            2 * plane + core,
+        )
+
+    def finish(weight, totals, moving, result):
+        for way, ok in ((0, z > 0), (1, z < last)):
+
+            @pl.when(ok)
+            def _():
+                arrive(moving.at[way, z], recv_rz.at[weight, way, z])
+                totals[z] += moving[way, z].astype(f32)
+
+        result[c] = totals[z].astype(bf)
         for slot in (3, 1, 2):
             push(result.at[c], result.at[c], send, recv_f.at[weight, slot], c ^ slot, f)
 
@@ -929,14 +970,17 @@
         left = jnp.concatenate([attq[b, shard] for b in range(4)], axis=1)
         return dot(left, gm[...].reshape(-1, gm.shape[2]))
 
+    far_rows(nt, recv_nt)
+    for slot in (1, 2, 3):
+        arrive(gpq.at[c ^ slot], recv_gp.at[slot])
+    sum_chip(1, produce_q, s_q, p_q, t_q)
+    chain(1, 0, t_q, o_q, z_q)
     for s in range(shards):
         part = dot(w_o[s], out_gm[...]).astype(bf)
         for j in range(per_shard):
             gp[per_shard * s + j] = paired(part[wide * j : wide * (j + 1)])
-    for slot in (1, 2, 3):
-        arrive(nt.at[c ^ slot], recv_nt.at[slot])
-        arrive(gpq.at[c ^ slot], recv_gp.at[slot])
-    sum_parts(1, produce_q, s_q, p_q, z_q, t_q)
+    chain(1, 1, t_q, o_q, z_q)
+    relay_rows(gm, recv_gm)
 
     def backward(g, carry):
         dk = jnp.zeros((DH, 4 * toks), f32)
@@ -954,7 +998,10 @@
         dkv_t[groups + g] = dv
         return carry
 
-    lax.fori_loop(0, groups, backward, 0)
+    lax.fori_loop(0, groups // 2, backward, 0)
+    for slot in slots[2:]:
+        chain(1, slot, t_q, o_q, z_q)
+    lax.fori_loop(groups // 2, groups, backward, 0)
     for b in range(4):
         for g in range(2 * groups):
             kvs[b, DH * g : DH * (g + 1)] = dkv_t[g, :, toks * b : toks * (b + 1)].astype(bf)
@@ -962,11 +1009,14 @@
         push(kvs.at[c ^ slot], kvr.at[slot], send, recv_kvs.at[slot], c ^ slot, f)
     for slot in (1, 2, 3):
         arrive(attq.at[c ^ slot], recv_att.at[slot])
-        arrive(gm.at[c ^ slot], recv_gm.at[slot])
-    sum_parts(0, produce_o, s_o, p_o, z_o, t_o)
+    far_rows(gm, recv_gm)
+    sum_chip(0, produce_o, s_o, p_o, t_o)
+    chain(0, 0, t_o, o_o, z_o)
     for i in range(pairs):
         out_dq[:, wide * i : wide * (i + 1)] = dqb_t[i].T
-    finish(1, z_q, t_q, res_q)
+    finish(1, t_q, z_q, res_q)
+    for slot in slots[1:]:
+        chain(0, slot, t_o, o_o, z_o)
     total = kvs[c].astype(f32)
     for slot in (1, 2, 3):
         arrive(kvr.at[slot], recv_kvs.at[slot])
@@ -974,12 +1024,15 @@
     total = total.astype(bf).T
     out_dk[...] = total[:, :kvd]
     out_dv[...] = total[:, kvd:]
-    finish(0, z_o, t_o, res_o)
+    finish(0, t_o, z_o, res_o)
     for weight, result in ((1, res_q), (0, res_o)):
         for slot in (3, 1, 2):
             arrive(result.at[c ^ slot], recv_f.at[weight, slot])
-    for copy in started:
-        copy.wait_send()
+    for when, copy in started:
+        if when is None:
+            copy.wait_send()
+        else:
+            pl.when(when)(copy.wait_send)
 
 
 def finish_kernel(b_in, gm_in, dq_in, dk_in, dv_in, o_in, q_in, b, gm, dq, dk, dv, wo, wq):
@@ -1066,8 +1119,9 @@
         scratch += [
             v((planes,) + part, bf),
             v((planes,) + part, bf),
-            v((2 * planes,) + part, bf),
-            v(part, f32),
+            v((planes,) + part, bf),
+            v((2, planes) + part, bf),
+            v((planes,) + part, f32),
         ]
     dma = pltpu.SemaphoreType.DMA
     scratch += [
@@ -1080,13 +1134,13 @@
         dma((2, planes)),
         dma((2, planes, 4)),
         dma((4,)),
-        dma((4,)),
+        dma((5,)),
         dma((2,)),
         dma((4,)),
-        dma((4,)),
+        dma((5,)),
         dma((4,)),
         dma((2, planes)),
-        dma((2, planes)),
+        dma((2, 2, planes)),
         dma((2, 4)),
     ]
     anywhere = pl.BlockSpec(memory_space=pl.ANY)

time: 172 us -> 152 us (0.88)
  the two profiles are of different devices: /device:TPU:14 before, /device:TPU:0 now
where the time goes in v2:
time: 152 us; the launch traced here: 151 us
  Pallas kernels  151 us (99%)
    pallas_call x1, Pallas kernels, one_kernel(): pl.pallas_call(functools.partial(mega_kernel, planes), out_shape=outs, in...  146 us
    pallas_call x1, Pallas kernels, one_kernel(): pl.pallas_call(finish_kernel, out_shape=final, in_specs=[in_vmem] * 7, ou...  4.38 us

profile of v2, /device:TPU:0, one launch (start us, length us, event | category | flops | bytes accessed | tf_op | source)
XLA Modules:
  0.0 151.4 jit_solution(15155796253203789373)
XLA Ops:
  0.6 146.4 %shard_map.144 = (bf16[128,2048]{1,0:T(8,128)(2,1)}, bf16[1440,128]{1,0:T(8,128)(2,1)}, bf16[128,2048]{1,0:T(8,128)(2,1)}, bf16[128,256]{1,0:T(8,128)(2,1)}, bf1...) custom-call(s32[1,6]{1,0:T(1,128)} %lens.1, bf16[128,2048]{1,0:T(8,128)(2,1)} %bitcast.20, ...), custom_call_target="tpu_custom_call" | custom-call | tf_op jit(solution)/shard_map/pallas_call | solution.py:1148
  147.1 4.4 %shard_map.145 = (bf16[128,2048]{1,0:T(8,128)(2,1)}, bf16[1440,128]{1,0:T(8,128)(2,1)}, bf16[128,2048]{1,0:T(8,128)(2,1)}, bf16[128,256]{1,0:T(8,128)(2,1)}, bf1...) custom-call(bf16[128,2048]{1,0:T(8,128)(2,1)} %get-tuple-element.21.b_in, ...), custom_call_target="tpu_custom_call" | custom-call | tf_op jit(solution)/shard_map/pallas_call | solution.py:1159

commit v3 on v2

--- a/solution.py
+++ b/solution.py
@@ -513,7 +513,8 @@
     out_dq,
     out_dk,
     out_dv,
-    res_o,
+    res_a,
+    res_b,
     res_q,
     q_v,
     resid_v,
@@ -563,11 +564,16 @@
     o_q,
     z_q,
     t_q,
-    s_o,
-    p_o,
-    o_o,
-    z_o,
-    t_o,
+    s_a,
+    p_a,
+    o_a,
+    z_a,
+    t_a,
+    s_b,
+    p_b,
+    o_b,
+    z_b,
+    t_b,
     local,
     send,
     recv_kv,
@@ -584,6 +590,7 @@
     recv_kvs,
     recv_rp,
     recv_rz,
+    recv_rq,
     recv_f,
 ):
     f32, bf = (jnp.float32, jnp.bfloat16)
@@ -614,8 +621,17 @@
 
     near = [sorted((s for s in range(planes) if s != i), key=lambda s: abs(s - i)) for i in range(planes)]
     sources = [by_plane(column) for column in zip(*near)]
-    targets = sources[::-1]
+    order = [
+        sorted(
+            (s for s in range(planes) if s != i),
+            key=lambda s: (i if s > i else planes - 1 - i, -abs(s - i)),
+        )
+        for i in range(planes)
+    ]
+    targets = [by_plane(column) for column in zip(*order)]
     last = planes - 1
+    edge = (z == 0) | (z == last)
+    between = (z > 0) & (z < last)
 
     def arrive(ref, sem):
         remote(ref, ref, send, sem, c ^ 1, f).wait_recv()
@@ -684,6 +700,7 @@
         push(mine, full[weight].at[f], send, recv_p.at[weight, 0, 0], c, f ^ 1)
 
     share(0)
+    share(1)
     steps = [(weight, d) for weight in (0, 1) for d in slots]
     count = len(steps)
 
@@ -802,8 +819,6 @@
 
     for g in range(groups):
         gather_step(g)
-        if g == 1:
-            share(1)
         forward(g)
     attq[c] = att_t[:, c // 2, pl.ds(pl.multiple_of(lax.rem(c, 2) * DH, DH), DH), :]
     for s in range(shards):
@@ -853,6 +868,16 @@
     ahead, behind = (lax.rem(c + 1, 4), lax.rem(c + 3, 4))
     push(kvx.at[1], kvx.at[0], send, recv_halo.at[0], ahead, f)
     share_rows(nt, recv_nt)
+    for slot in (1, 2, 3):
+        peer = c ^ slot
+        push(
+            att_t.at[:, peer // 2, pl.ds(pl.multiple_of(lax.rem(peer, 2) * DH, DH), DH), :],
+            attq.at[c],
+            send,
+            recv_att.at[slot],
+            peer,
+            f,
+        )
     for i in range(pairs):
         qb[i] = scaled(paired(acc_p[:, wide * i : wide * (i + 1)].astype(bf).T))
     arrive(kvx.at[0], recv_halo.at[0])
@@ -909,16 +934,6 @@
     grad_mid = gr_v[...].astype(f32).T + change
     gm[c] = grad_mid.astype(bf)
     share_rows(gm, recv_gm)
-    for slot in (1, 2, 3):
-        peer = c ^ slot
-        push(
-            att_t.at[:, peer // 2, pl.ds(pl.multiple_of(lax.rem(peer, 2) * DH, DH), DH), :],
-            attq.at[c],
-            send,
-            recv_att.at[slot],
-            peer,
-            f,
-        )
     out_gm[...] = gm[c].T
 
     def sum_chip(weight, produce, sent, from_p, totals):
@@ -930,17 +945,15 @@
             arrive(from_p.at[d], recv_rp.at[weight, d])
             totals[d] = mine + from_p[d].astype(f32)
 
-    def chain(weight, slot, totals, out, moving):
+    def spread_result(weight, value, result):
+        result[c] = value.astype(bf)
+        for slot in (3, 1, 2):
+            push(result.at[c], result.at[c], send, recv_f.at[weight, slot], c ^ slot, f)
+
+    def onward(weight, slot, out, moving, ok):
         target = targets[slot]
         way = jnp.where(target > z, 0, 1)
         plane = jnp.where(target > z, z + 1, z - 1)
-
-        @pl.when(jnp.where(target > z, z > 0, z < last))
-        def _():
-            arrive(moving.at[way, target], recv_rz.at[weight, way, target])
-            totals[target] += moving[way, target].astype(f32)
-
-        out[slot] = totals[target].astype(bf)
         push(
             out.at[slot],
             moving.at[way, target],
@@ -948,7 +961,48 @@
             recv_rz.at[weight, way, target],
             c,
             2 * plane + core,
+            when=ok,
         )
+
+    def direct(totals, out, moving):
+        for slot in slots:
+            target = sources[::-1][slot]
+            out[slot] = totals[target].astype(bf)
+            push(
+                out.at[slot],
+                moving.at[0, z],
+                send,
+                recv_rq.at[z],
+                c,
+                2 * target + core,
+            )
+
+    def finish_direct(totals, moving, result):
+        value = totals[z]
+        for source in sources:
+            arrive(moving.at[0, source], recv_rq.at[source])
+            value += moving[0, source].astype(f32)
+        spread_result(1, value, result)
+
+    def ends_send(weight, send_slots, totals, out, moving):
+        for slot in send_slots:
+
+            @pl.when(edge)
+            def _():
+                out[slot] = totals[targets[slot]].astype(bf)
+
+            onward(weight, slot, out, moving, edge)
+
+    def chain(weight, slot, totals, out, moving):
+        target = targets[slot]
+        way = jnp.where(target > z, 0, 1)
+
+        @pl.when(between)
+        def _():
+            arrive(moving.at[way, target], recv_rz.at[weight, way, target])
+            out[slot] = (totals[target] + moving[way, target].astype(f32)).astype(bf)
+
+        onward(weight, slot, out, moving, between)
 
     def finish(weight, totals, moving, result):
         for way, ok in ((0, z > 0), (1, z < last)):
@@ -958,30 +1012,27 @@
                 arrive(moving.at[way, z], recv_rz.at[weight, way, z])
                 totals[z] += moving[way, z].astype(f32)
 
-        result[c] = totals[z].astype(bf)
-        for slot in (3, 1, 2):
-            push(result.at[c], result.at[c], send, recv_f.at[weight, slot], c ^ slot, f)
+        spread_result(weight, totals[z], result)
 
     def produce_q(shard):
         left = jnp.concatenate([nt[b, shard] for b in range(4)], axis=1)
         return dot(left, gpq[...].reshape(-1, gp_width))
 
-    def produce_o(shard):
+    def produce_o(low, high, shard):
         left = jnp.concatenate([attq[b, shard] for b in range(4)], axis=1)
-        return dot(left, gm[...].reshape(-1, gm.shape[2]))
-
-    far_rows(nt, recv_nt)
-    for slot in (1, 2, 3):
-        arrive(gpq.at[c ^ slot], recv_gp.at[slot])
-    sum_chip(1, produce_q, s_q, p_q, t_q)
-    chain(1, 0, t_q, o_q, z_q)
+        return dot(left, gm[:, :, low:high].reshape(-1, high - low))
+
+    split = res_a.shape[2]
+    produce_a = functools.partial(produce_o, 0, split)
+    produce_b = functools.partial(produce_o, split, gm.shape[2])
+    for_q = (t_q, o_q, z_q)
+    for_a = (t_a, o_a, z_a)
+    for_b = (t_b, o_b, z_b)
+
     for s in range(shards):
         part = dot(w_o[s], out_gm[...]).astype(bf)
         for j in range(per_shard):
             gp[per_shard * s + j] = paired(part[wide * j : wide * (j + 1)])
-    chain(1, 1, t_q, o_q, z_q)
-    relay_rows(gm, recv_gm)
-
     def backward(g, carry):
         dk = jnp.zeros((DH, 4 * toks), f32)
         dv = jnp.zeros((DH, 4 * toks), f32)
@@ -999,8 +1050,12 @@
         return carry
 
     lax.fori_loop(0, groups // 2, backward, 0)
-    for slot in slots[2:]:
-        chain(1, slot, t_q, o_q, z_q)
+    far_rows(nt, recv_nt)
+    for slot in (1, 2, 3):
+        arrive(gpq.at[c ^ slot], recv_gp.at[slot])
+    sum_chip(1, produce_q, s_q, p_q, t_q)
+    direct(*for_q)
+    relay_rows(gm, recv_gm)
     lax.fori_loop(groups // 2, groups, backward, 0)
     for b in range(4):
         for g in range(2 * groups):
@@ -1010,13 +1065,21 @@
     for slot in (1, 2, 3):
         arrive(attq.at[c ^ slot], recv_att.at[slot])
     far_rows(gm, recv_gm)
-    sum_chip(0, produce_o, s_o, p_o, t_o)
-    chain(0, 0, t_o, o_o, z_o)
+    sum_chip(0, produce_a, s_a, p_a, t_a)
+    ends_send(0, slots[:1], *for_a)
+    sum_chip(2, produce_b, s_b, p_b, t_b)
+    for slot in slots:
+        if slot:
+            ends_send(0, slots[slot : slot + 1], *for_a)
+        ends_send(2, slots[slot : slot + 1], *for_b)
     for i in range(pairs):
         out_dq[:, wide * i : wide * (i + 1)] = dqb_t[i].T
-    finish(1, t_q, z_q, res_q)
+    finish_direct(t_q, z_q, res_q)
+    chain(0, 0, *for_a)
+    chain(2, 0, *for_b)
     for slot in slots[1:]:
-        chain(0, slot, t_o, o_o, z_o)
+        chain(0, slot, *for_a)
+        chain(2, slot, *for_b)
     total = kvs[c].astype(f32)
     for slot in (1, 2, 3):
         arrive(kvr.at[slot], recv_kvs.at[slot])
@@ -1024,8 +1087,9 @@
     total = total.astype(bf).T
     out_dk[...] = total[:, :kvd]
     out_dv[...] = total[:, kvd:]
-    finish(0, t_o, z_o, res_o)
-    for weight, result in ((1, res_q), (0, res_o)):
+    finish(0, t_a, z_a, res_a)
+    finish(2, t_b, z_b, res_b)
+    for weight, result in ((1, res_q), (0, res_a), (2, res_b)):
         for slot in (3, 1, 2):
             arrive(result.at[c ^ slot], recv_f.at[weight, slot])
     for when, copy in started:
@@ -1035,14 +1099,15 @@
             pl.when(when)(copy.wait_send)
 
 
-def finish_kernel(b_in, gm_in, dq_in, dk_in, dv_in, o_in, q_in, b, gm, dq, dk, dv, wo, wq):
+def finish_kernel(b_in, gm_in, dq_in, dk_in, dv_in, oa, ob, q_in, b, gm, dq, dk, dv, wo, wq):
     for src, dst in ((b_in, b), (gm_in, gm), (dq_in, dq), (dk_in, dk), (dv_in, dv)):
         dst[...] = src[...]
     width = q_in.shape[2]
     for quarter in range(4):
         wq[:, width * quarter : width * (quarter + 1)] = q_in[quarter].astype(jnp.float32)
-    whole = o_in[...].reshape(-1, o_in.shape[2]).astype(jnp.float32)
-    wo[...] = whole.T
+    split = oa.shape[2]
+    wo[:split] = oa[...].reshape(-1, split).astype(jnp.float32).T
+    wo[split:] = ob[...].reshape(-1, ob.shape[2]).astype(jnp.float32).T
 
 
 def one_kernel(lengths, query, keys, values, resid, w_out, w_qkv, grad_out, grad_resid):
@@ -1059,14 +1124,17 @@
     groups = kvd // DH
     seq = 4 * toks
     shape = jax.ShapeDtypeStruct
-    o_part, q_part = ((rows_o // 4, dim), (rows_q, width // 4))
+    split = (dim // 256 + 1) * 128
+    a_part, b_part = ((rows_o // 4, split), (rows_o // 4, dim - split))
+    q_part = (rows_q, width // 4)
     outs = (
         shape((toks, hd), bf),
         shape((dim, toks), bf),
         shape((toks, hd), bf),
         shape((toks, kvd), bf),
         shape((toks, kvd), bf),
-        shape((4,) + o_part, bf),
+        shape((4,) + a_part, bf),
+        shape((4,) + b_part, bf),
         shape((4,) + q_part, bf),
     )
     v = pltpu.VMEM
@@ -1115,7 +1183,7 @@
         v((4, 2 * kvd, toks), bf),
         v((4, 2 * kvd, toks), bf),
     ]
-    for part in (q_part, o_part):
+    for part in (q_part, a_part, b_part):
         scratch += [
             v((planes,) + part, bf),
             v((planes,) + part, bf),
@@ -1139,9 +1207,10 @@
         dma((4,)),
         dma((5,)),
         dma((4,)),
-        dma((2, planes)),
-        dma((2, 2, planes)),
-        dma((2, 4)),
+        dma((3, planes)),
+        dma((3, 2, planes)),
+        dma((planes,)),
+        dma((3, 4)),
     ]
     anywhere = pl.BlockSpec(memory_space=pl.ANY)
     in_vmem = pl.BlockSpec(memory_space=pltpu.VMEM)
@@ -1149,7 +1218,7 @@
         functools.partial(mega_kernel, planes),
         out_shape=outs,
         in_specs=[pl.BlockSpec(memory_space=pltpu.SMEM)] + [anywhere] * 8,
-        out_specs=(in_vmem,) * 7,
+        out_specs=(in_vmem,) * 8,
         scratch_shapes=scratch,
         compiler_params=pltpu.CompilerParams(
             collective_id=0, has_side_effects=True, vmem_limit_bytes=60 * 2**20
@@ -1159,7 +1228,7 @@
     b, gm, dq, dk, dv, wo, wq = pl.pallas_call(
         finish_kernel,
         out_shape=final,
-        in_specs=[in_vmem] * 7,
+        in_specs=[in_vmem] * 8,
         out_specs=(in_vmem,) * 7,
     )(*results)
     return (b[None], gm.T[None], dq[None], dk[None], dv[None], wo.T, wq)

time: 152 us -> 147 us (0.967)
  Pallas kernels: 151 us -> 146 us
    pallas_call x1, Pallas kernels: 146 us -> 142 us  [one_kernel(): pl.pallas_call(functools.partial(mega_kernel, planes), out_shape=outs, in...]
where the time goes in v3:
time: 147 us
  Pallas kernels  146 us (99%)
    pallas_call x1, Pallas kernels, one_kernel(): pl.pallas_call(functools.partial(mega_kernel, planes), out_shape=outs, in...  142 us
    pallas_call x1, Pallas kernels, one_kernel(): pl.pallas_call(finish_kernel, out_shape=final, in_specs=[in_vmem] * 8, ou...  4.39 us

profile of v3, /device:TPU:0, one launch (start us, length us, event | category | flops | bytes accessed | tf_op | source)
XLA Modules:
  0.0 147.1 jit_solution(12011494768760514904)
XLA Ops:
  0.6 142.1 %shard_map.144 = (bf16[128,2048]{1,0:T(8,128)(2,1)}, bf16[1440,128]{1,0:T(8,128)(2,1)}, bf16[128,2048]{1,0:T(8,128)(2,1)}, bf16[128,256]{1,0:T(8,128)(2,1)}, bf1...) custom-call(s32[1,6]{1,0:T(1,128)} %lens.1, ...), custom_call_target="tpu_custom_call" | custom-call | tf_op jit(solution)/shard_map/pallas_call | solution.py:1217
  142.7 4.4 %shard_map.145 = (bf16[128,2048]{1,0:T(8,128)(2,1)}, bf16[1440,128]{1,0:T(8,128)(2,1)}, bf16[128,2048]{1,0:T(8,128)(2,1)}, bf16[128,256]{1,0:T(8,128)(2,1)}, bf1...) custom-call(bf16[128,2048]{1,0:T(8,128)(2,1)} %get-tuple-element.22.b_in, ...), custom_call_target="tpu_custom_call" | custom-call | tf_op jit(solution)/shard_map/pallas_call | solution.py:1228
